TPU v7x, 128 devices: a whole 4x4x4 slice. The times are simulated.
128 devices in a mesh: band: 32 (over y, x_hi, z), grid: 4 (over x_lo, core).
Axes of the slice: x: 4 (x_hi: 2, x_lo: 2; x = x_hi * 2 + x_lo), y: 4, z: 4, core: 2. Of those that a mesh axis runs over, the one named last changes fastest.
Arguments:
- orbitals: float32 [96, 64, 4096], P('band', 'grid'), may hold values from -6 to 6
- pair_mask: int32 [96, 96], replicated, may hold values from 0 to 1, as said below
Outputs:
- exchange_term: float32 [96, 64, 4096], P('band', 'grid')
Inputs may be any that keep to these rules, and one draw needn't show every extreme that they name: pair_mask is symmetric; entries outside the candidate pairs of every block (and their transposes) are 0; each block has at most 12 candidate pairs with mask 1, and some block has exactly 12.
All inputs are finite; a program needn't handle non-finite values.
Results may differ from a plain program's by a relative error of at most 0.00027.
Values sent between devices are 32-bit elements; how exact they have to be, the bound alone decides.
A program may use at most 64 MiB of HBM per device.

v0:
```python
import math

import jax
import jax.numpy as jnp
import numpy as np
from jax import lax
from jax.sharding import PartitionSpec as P

NG = 64
ORB_DEV = 3
REACH = 2
NCAND = 24
CAP = 12


MIXING = 0.25
BOX_LENGTH = 16.0
EXACT_PRECISION = lax.Precision.HIGHEST
turn_pairs = 4


def shifted(block, axis, distance):
    devices = range(lax.axis_size(axis))
    route = [((i - distance) % len(devices), i) for i in devices]
    return lax.ppermute(block, axis, route)


def pair_table():
    entries = []
    for distance in range(REACH + 1):
        for leading_orbital in range(ORB_DEV):
            for second_orb in range(ORB_DEV):
                if distance > 0 or leading_orbital <= second_orb:
                    entries.append((leading_orbital, distance, second_orb))
    return np.array(entries, dtype=np.int32)


def dft_tables(length):
    positions = jnp.arange(length, dtype=jnp.int32)
    product_mod = positions[:, None] * positions[None, :] % length
    angles = product_mod.astype(jnp.float32) * (2.0 * math.pi / length)
    return (jnp.cos(angles), jnp.sin(angles))


def rotate_parts(values_in):
    half_width = values_in.shape[-1] // 2
    return jnp.concatenate([values_in[..., half_width:], -values_in[..., :half_width]], axis=-1)


def transform_axis(values_in, tables, formula, sweep_direction):
    cosine_table, sine_table = tables
    direct_part = jnp.einsum(formula, cosine_table, values_in, precision=EXACT_PRECISION)
    crossed_part = jnp.einsum(formula, sine_table, values_in, precision=EXACT_PRECISION)
    return direct_part + sweep_direction * rotate_parts(crossed_part)


def signed_frequency(positions):
    return jnp.where(positions < NG // 2, positions, positions - NG)


def coulomb_values(squared):
    safe_values = jnp.maximum(squared, 1).astype(jnp.float32)
    return jnp.where(squared > 0, BOX_LENGTH * BOX_LENGTH / math.pi / safe_values, 0.0)


def solve_poisson(density, tables, kernel_pair, z_tables):
    count_pairs = density.shape[0]
    planes = density.shape[1]
    cubes = density.reshape(count_pairs, planes, NG, NG)
    joined = jnp.concatenate([cubes[0::2], cubes[1::2]], axis=-1)
    spectrum = jnp.einsum("pxyz,zk->pxyk", joined, z_tables[0], precision=EXACT_PRECISION)
    spectrum = transform_axis(spectrum, tables, "ky,pxyc->pxkc", 1.0)
    columns = lax.all_to_all(spectrum, "grid", split_axis=2, concat_axis=1, tiled=True)
    columns = transform_axis(columns, tables, "kx,pxyc->pkyc", 1.0)
    columns = columns * kernel_pair[None]
    columns = transform_axis(columns, tables, "kx,pxyc->pkyc", -1.0)
    returned = lax.all_to_all(columns, "grid", split_axis=1, concat_axis=2, tiled=True)
    returned = transform_axis(returned, tables, "ky,pxyc->pxkc", -1.0)
    fields = jnp.einsum("pxyc,ck->pxyk", returned, z_tables[2], precision=EXACT_PRECISION)
    potential = jnp.stack([fields[..., :NG], fields[..., NG:]], axis=1)
    return potential.reshape(count_pairs, planes, NG * NG)


def local(orbitals, pair_mask):
    orb_count, planes, cells = orbitals.shape
    groups = lax.axis_size("band")
    band_index = lax.axis_index("band")
    grid_index = lax.axis_index("grid")
    visits = [orbitals]
    for distance in range(1, REACH + 1):
        visits.append(shifted(orbitals, "band", -distance))
    flat_count = (REACH + 1) * orb_count
    flat_visiting = jnp.stack(visits).reshape(flat_count, planes, cells)
    pair_list = pair_table()
    first_ids = jnp.asarray(pair_list[:, 0])
    offsets = jnp.asarray(pair_list[:, 1])
    second_ids = jnp.asarray(pair_list[:, 2])
    row_ids = band_index * ORB_DEV + first_ids
    col_ids = (band_index + offsets) % groups * ORB_DEV + second_ids
    live_flags = pair_mask[row_ids, col_ids]
    sort_keys = (1 - live_flags) * NCAND + jnp.arange(NCAND, dtype=jnp.int32)
    live_order = jnp.argsort(sort_keys)[:CAP]
    first_ids = first_ids[live_order]
    offsets = offsets[live_order]
    second_ids = second_ids[live_order]
    live_flags = live_flags[live_order]
    padding = -first_ids.shape[0] % turn_pairs

    def padded(values_in):
        return jnp.concatenate([values_in, jnp.zeros((padding,), jnp.int32)])

    first_ids = padded(first_ids)
    offsets = padded(offsets)
    second_ids = padded(second_ids)
    live_flags = padded(live_flags)
    slot_ids = offsets * ORB_DEV + second_ids
    weights = live_flags.astype(jnp.float32)
    self_flags = 1.0 - ((offsets == 0) & (first_ids == second_ids)).astype(jnp.float32)
    turns = first_ids.shape[0] // turn_pairs
    tables = dft_tables(NG)
    cosine_table, sine_table = tables
    forward_complex = jnp.block([[cosine_table, -sine_table], [sine_table, cosine_table]])
    forward_real = jnp.concatenate([cosine_table, -sine_table], axis=1)
    inverse_complex = jnp.block([[cosine_table, sine_table], [-sine_table, cosine_table]])
    inverse_real = jnp.concatenate([cosine_table, -sine_table], axis=0)
    z_tables = (forward_complex, forward_real, inverse_complex, inverse_real)
    waves_first = signed_frequency(jnp.arange(NG, dtype=jnp.int32))[:, None, None]
    waves_second = signed_frequency(grid_index * planes + jnp.arange(planes, dtype=jnp.int32))[
        None, :, None
    ]
    waves_third = signed_frequency(jnp.arange(NG, dtype=jnp.int32))[None, None, :]
    kernel = coulomb_values(
        waves_first * waves_first + waves_second * waves_second + waves_third * waves_third
    ) / float(NG**3)
    kernel_pair = jnp.concatenate([kernel, kernel], axis=-1)

    def one_turn(totals, turn_input):
        owned_total, visit_total = totals
        first_turn, slot_turn, weight_turn, self_turn = turn_input
        leading_orbital = orbitals[first_turn]
        second_orb = flat_visiting[slot_turn]
        potential = solve_poisson(leading_orbital * second_orb, tables, kernel_pair, z_tables)
        weighted_density = potential * weight_turn[:, None, None]
        owner_hot = (first_turn[:, None] == jnp.arange(orb_count, dtype=jnp.int32)[None, :]).astype(
            jnp.float32
        )
        visit_onehot_mask = (
            slot_turn[:, None] == jnp.arange(flat_count, dtype=jnp.int32)[None, :]
        ).astype(jnp.float32) * self_turn[:, None]
        owned_total = owned_total + jnp.einsum(
            "pa,pxc->axc", owner_hot, weighted_density * second_orb, precision=EXACT_PRECISION
        )
        visit_total = visit_total + jnp.einsum(
            "sq,swt->qwt",
            visit_onehot_mask,
            weighted_density * leading_orbital,
            precision=EXACT_PRECISION,
        )
        return ((owned_total, visit_total), None)

    start_totals = (
        jnp.zeros((orb_count, planes, cells), jnp.float32),
        jnp.zeros((flat_count, planes, cells), jnp.float32),
    )
    turn_inputs = (
        first_ids.reshape(turns, turn_pairs),
        slot_ids.reshape(turns, turn_pairs),
        weights.reshape(turns, turn_pairs),
        self_flags.reshape(turns, turn_pairs),
    )
    (owned_total, visit_total), discarded_value = lax.scan(one_turn, start_totals, turn_inputs)
    visit_total = visit_total.reshape(REACH + 1, orb_count, planes, cells)
    owned = owned_total + visit_total[0]
    for distance in range(1, REACH + 1):
        owned = owned + shifted(visit_total[distance], "band", distance)
    return -MIXING * owned


def solution(mesh):
    return jax.shard_map(
        local,
        mesh=mesh,
        in_specs=(P("band", "grid", None), P()),
        out_specs=P("band", "grid", None),
        check_vma=False,
    )
```

profile of v0, /device:TPU:1, one launch (start us, length us, event | category | flops | bytes accessed | tf_op | source)
XLA Modules:
  0.0 318.7 jit_solution(15074602083450062132)
XLA Ops:
  0.0 9.3 %collective-permute-start.1 = (f32[3,16,4096]{2,1,0:T(8,128)}, f32[3,16,4096]{2,1,0:T(8,128)S(1)}, u32[]{:S(2)}, u32[]{:S(2)}) collective-permute-start(f32[3,16,4096]{2,1,0:T(8,128)} %param.7), channel_id=1, source_target_pairs={{8,0},{12,4},{16,8},{20,12},{24,16},{28,20},{32,24},{36,28},{40,32... | collective-permute-start | bytes 2359304 | tf_op jit(solution)/shard_map/ppermute | solution.py:25
  19.7 6.2 %collective-permute-done.1 = f32[3,16,4096]{2,1,0:T(8,128)S(1)} collective-permute-done((f32[3,16,4096]{2,1,0:T(8,128)}, f32[3,16,4096]{2,1,0:T(8,128)S(1)}, u32[]{:S(2)}, u32[]{:S(2)}) %collective-permute-start.1) | collective-permute-done | bytes 786464 | tf_op jit(solution)/shard_map/ppermute | solution.py:25
  25.9 17.2 %collective-permute-done = f32[3,16,4096]{2,1,0:T(8,128)S(1)} collective-permute-done((f32[3,16,4096]{2,1,0:T(8,128)}, f32[3,16,4096]{2,1,0:T(8,128)S(1)}, u32[]{:S(2)}, u32[]{:S(2)}) %collective-permute-start) | collective-permute-done | bytes 786464 | tf_op jit(solution)/shard_map/ppermute | solution.py:25
  44.8 226.9 %while.14 = (s32[]{:T(128)}, f32[3,16,4096]{2,0,1:T(4,128)}, f32[9,16,4096]{2,0,1:T(8,128)}, s32[3,4]{1,0:T(4,128)S(1)}, f32[3,16,4096]{2,1,0:T(8,128)S(1)}, /*i...) while((s32[]{:T(128)}, f32[3,16,4096]{2,0,1:T(4,128)}, ...), condition=%wide.region_2.3_spmd.clone.clone, body=%wide.region_1.2_spmd.clone.clone.sunk | while | flops 2460682240 | bytes 111813288 | solution.py:171
  45.4 2.3 gather_fusion.1
  47.8 2.2 mul.862
  56.4 17.3 %all_to_all.48 = f32[2,16,64,128]{3,1,0,2:T(8,128)S(1)} all-to-all(f32[2,16,64,128]{3,1,0,2:T(8,128)S(1)} %copy.52), channel_id=1, replica_groups=mesh['band'=32,'grid'=4] {'grid'}, dimensions={2} | all-to-all | bytes 2097152 | tf_op jit(solution)/shard_map/while/body/eval_jaxpr/all_to_all | solution.py:73
  82.3 4.5 %all-to-all-start.1 = ((f32[2,64,16,128]{3,2,0,1:T(8,128)}), f32[2,64,16,128]{3,2,0,1:T(8,128)S(1)}, u32[]{:S(2)}, u32[]{:S(2)}) async-start(f32[2,64,16,128]{3,2,0,1:T(8,128)} %copy.54), calls=%async_computation.1 | async-start | bytes 2097152 | tf_op jit(solution)/shard_map/while/body/eval_jaxpr/all_to_all | solution.py:77
  86.8 13.5 %all-to-all-done.1 = f32[2,64,16,128]{3,2,0,1:T(8,128)S(1)} async-done(((f32[2,64,16,128]{3,2,0,1:T(8,128)}), f32[2,64,16,128]{3,2,0,1:T(8,128)S(1)}, u32[]{:S(2)}, u32[]{:S(2)}) %all-to-all-start.1) | async-done | bytes 1048608 | tf_op jit(solution)/shard_map/while/body/eval_jaxpr/all_to_all | solution.py:77
  106.6 2.1 reshape.255
  109.9 2.5 convolution_add_fusion.4
  112.4 6.4 %convolution_add_fusion.5 = f32[9,16,4096]{2,0,1:T(8,128)S(1)} fusion(f32[9,16,4096]{2,0,1:T(8,128)S(1)} %copy-done.1, pred[]{:T(512)S(6)} %compare.9, f32[4,16,4096]{2,1,0:T(8,128)S(1)} %get-tuple-element.342, f32[4]{0:T(128)S(1)} %get-tuple-element.343, s32[4]{0:T(128)S(1)} %get-tuple-element.344), kind=kOutput, calls=%fused_computation.9.clone.1 | convolution fusion | flops 29491272 | bytes 5767201 | tf_op jit(solution)/shard_map/while/body/eval_jaxpr/sq,swt->qwt/dot_general | solution.py:153
  118.8 1.9 copy-done.2
  121.4 2.3 gather_fusion.1
  123.8 2.2 mul.862
  132.4 16.8 %all_to_all.48 = f32[2,16,64,128]{3,1,0,2:T(8,128)S(1)} all-to-all(f32[2,16,64,128]{3,1,0,2:T(8,128)S(1)} %copy.52), channel_id=1, replica_groups=mesh['band'=32,'grid'=4] {'grid'}, dimensions={2} | all-to-all | bytes 2097152 | tf_op jit(solution)/shard_map/while/body/eval_jaxpr/all_to_all | solution.py:73
  157.7 4.5 %all-to-all-start.1 = ((f32[2,64,16,128]{3,2,0,1:T(8,128)}), f32[2,64,16,128]{3,2,0,1:T(8,128)S(1)}, u32[]{:S(2)}, u32[]{:S(2)}) async-start(f32[2,64,16,128]{3,2,0,1:T(8,128)} %copy.54), calls=%async_computation.1 | async-start | bytes 2097152 | tf_op jit(solution)/shard_map/while/body/eval_jaxpr/all_to_all | solution.py:77
  162.2 13.5 %all-to-all-done.1 = f32[2,64,16,128]{3,2,0,1:T(8,128)S(1)} async-done(((f32[2,64,16,128]{3,2,0,1:T(8,128)}), f32[2,64,16,128]{3,2,0,1:T(8,128)S(1)}, u32[]{:S(2)}, u32[]{:S(2)}) %all-to-all-start.1) | async-done | bytes 1048608 | tf_op jit(solution)/shard_map/while/body/eval_jaxpr/all_to_all | solution.py:77
  182.0 2.1 reshape.255
  185.4 2.5 convolution_add_fusion.4
  187.9 6.4 %convolution_add_fusion.5 = f32[9,16,4096]{2,0,1:T(8,128)S(1)} fusion(f32[9,16,4096]{2,0,1:T(8,128)S(1)} %copy-done.1, pred[]{:T(512)S(6)} %compare.9, f32[4,16,4096]{2,1,0:T(8,128)S(1)} %get-tuple-element.342, f32[4]{0:T(128)S(1)} %get-tuple-element.343, s32[4]{0:T(128)S(1)} %get-tuple-element.344), kind=kOutput, calls=%fused_computation.9.clone.1 | convolution fusion | flops 29491272 | bytes 5767201 | tf_op jit(solution)/shard_map/while/body/eval_jaxpr/sq,swt->qwt/dot_general | solution.py:153
  196.9 2.3 gather_fusion.1
  199.3 2.2 mul.862
  207.9 16.8 %all_to_all.48 = f32[2,16,64,128]{3,1,0,2:T(8,128)S(1)} all-to-all(f32[2,16,64,128]{3,1,0,2:T(8,128)S(1)} %copy.52), channel_id=1, replica_groups=mesh['band'=32,'grid'=4] {'grid'}, dimensions={2} | all-to-all | bytes 2097152 | tf_op jit(solution)/shard_map/while/body/eval_jaxpr/all_to_all | solution.py:73
  233.1 4.5 %all-to-all-start.1 = ((f32[2,64,16,128]{3,2,0,1:T(8,128)}), f32[2,64,16,128]{3,2,0,1:T(8,128)S(1)}, u32[]{:S(2)}, u32[]{:S(2)}) async-start(f32[2,64,16,128]{3,2,0,1:T(8,128)} %copy.54), calls=%async_computation.1 | async-start | bytes 2097152 | tf_op jit(solution)/shard_map/while/body/eval_jaxpr/all_to_all | solution.py:77
  237.7 13.5 %all-to-all-done.1 = f32[2,64,16,128]{3,2,0,1:T(8,128)S(1)} async-done(((f32[2,64,16,128]{3,2,0,1:T(8,128)}), f32[2,64,16,128]{3,2,0,1:T(8,128)S(1)}, u32[]{:S(2)}, u32[]{:S(2)}) %all-to-all-start.1) | async-done | bytes 1048608 | tf_op jit(solution)/shard_map/while/body/eval_jaxpr/all_to_all | solution.py:77
  257.5 2.1 reshape.255
  260.8 2.5 convolution_add_fusion.4
  263.3 6.4 %convolution_add_fusion.5 = f32[9,16,4096]{2,0,1:T(8,128)S(1)} fusion(f32[9,16,4096]{2,0,1:T(8,128)S(1)} %copy-done.1, pred[]{:T(512)S(6)} %compare.9, f32[4,16,4096]{2,1,0:T(8,128)S(1)} %get-tuple-element.342, f32[4]{0:T(128)S(1)} %get-tuple-element.343, s32[4]{0:T(128)S(1)} %get-tuple-element.344), kind=kOutput, calls=%fused_computation.9.clone.1 | convolution fusion | flops 29491272 | bytes 5767201 | tf_op jit(solution)/shard_map/while/body/eval_jaxpr/sq,swt->qwt/dot_general | solution.py:153
  271.6 3.6 %copy.30 = f32[9,16,4096]{2,1,0:T(8,128)S(1)} copy(f32[9,16,4096]{2,0,1:T(8,128)} %get-tuple-element.394) | data formatting | bytes 4718592 | tf_op jit(solution)/shard_map/while | solution.py:171
  277.1 22.5 %collective-permute-done.3 = f32[3,16,4096]{2,1,0:T(8,128)S(1)} collective-permute-done((f32[3,16,4096]{2,1,0:T(8,128)S(1)}, f32[3,16,4096]{2,1,0:T(8,128)S(1)}, u32[]{:S(2)}, u32[]{:S(2)}) %collective-permute-start.3) | collective-permute-done | bytes 786464 | tf_op jit(solution)/shard_map/ppermute | solution.py:25
  299.5 17.6 %collective-permute-done.2 = f32[3,16,4096]{2,1,0:T(8,128)S(1)} collective-permute-done((f32[3,16,4096]{2,1,0:T(8,128)S(1)}, f32[3,16,4096]{2,1,0:T(8,128)S(1)}, u32[]{:S(2)}, u32[]{:S(2)}) %collective-permute-start.2) | collective-permute-done | bytes 786464 | tf_op jit(solution)/shard_map/ppermute | solution.py:25
  (168 shorter events, 88.1 us)
Async XLA Ops:
  0.0 10.5 %copy-start = (s32[96,96]{1,0:T(8,128)S(1)}, s32[96,96]{1,0:T(8,128)}, u32[]{:S(2)}) copy-start(s32[96,96]{1,0:T(8,128)} %param.8) | copy-start | bytes 110596
  0.0 43.1 %copy-start.3 = (f32[3,16,4096]{2,1,0:T(8,128)S(1)}, f32[3,16,4096]{2,1,0:T(8,128)}, u32[]{:S(2)}) copy-start(f32[3,16,4096]{2,1,0:T(8,128)} %param.7) | copy-start | bytes 2359300
  0.0 25.9 %collective-permute-start.1 = (f32[3,16,4096]{2,1,0:T(8,128)}, f32[3,16,4096]{2,1,0:T(8,128)S(1)}, u32[]{:S(2)}, u32[]{:S(2)}) collective-permute-start(f32[3,16,4096]{2,1,0:T(8,128)} %param.7), channel_id=1, source_target_pairs={{8,0},{12,4},{16,8},{20,12},{24,16},{28,20},{32,24},{36,28},{40,32... | collective-permute-start | bytes 2359304 | tf_op jit(solution)/shard_map/ppermute | solution.py:25
  9.3 33.8 %collective-permute-start = (f32[3,16,4096]{2,1,0:T(8,128)}, f32[3,16,4096]{2,1,0:T(8,128)S(1)}, u32[]{:S(2)}, u32[]{:S(2)}) collective-permute-start(f32[3,16,4096]{2,1,0:T(8,128)} %param.7), channel_id=1, source_target_pairs={{4,0},{8,4},{12,8},{16,12},{20,16},{24,20},{28,24},{32,28},{36,32}... | collective-permute-start | bytes 2359304 | tf_op jit(solution)/shard_map/ppermute | solution.py:25
  75.1 1.0 copy-start.8
  82.3 18.0 %all-to-all-start.1 = ((f32[2,64,16,128]{3,2,0,1:T(8,128)}), f32[2,64,16,128]{3,2,0,1:T(8,128)S(1)}, u32[]{:S(2)}, u32[]{:S(2)}) async-start(f32[2,64,16,128]{3,2,0,1:T(8,128)} %copy.54), calls=%async_computation.1 | async-start | bytes 2097152 | tf_op jit(solution)/shard_map/while/body/eval_jaxpr/all_to_all | solution.py:77
  108.7 1.2 copy-start.5
  108.7 3.7 %copy-start.1 = (f32[9,16,4096]{2,0,1:T(8,128)S(1)}, f32[9,16,4096]{2,0,1:T(8,128)}, u32[]{:S(2)}) copy-start(f32[9,16,4096]{2,0,1:T(8,128)} %get-tuple-element.361) | copy-start | bytes 7077892 | tf_op jit(solution)/shard_map/while
  112.4 6.4 %copy-start.6 = (f32[3,16,4096]{2,0,1:T(4,128)}, f32[3,16,4096]{2,0,1:T(4,128)S(1)}, u32[]{:S(2)}) copy-start(f32[3,16,4096]{2,0,1:T(4,128)S(1)} %convolution_add_fusion.4) | copy-start | bytes 2359300 | tf_op jit(solution)/shard_map/while
  112.4 8.4 %copy-start.4 = (f32[3,16,4096]{2,1,0:T(8,128)S(1)}, f32[3,16,4096]{2,1,0:T(8,128)}, u32[]{:S(2)}) copy-start(f32[3,16,4096]{2,1,0:T(8,128)} %get-tuple-element.406) | copy-start | bytes 2359300 | tf_op jit(solution)/shard_map/while
  118.8 1.9 copy-start.2
  150.5 1.0 copy-start.8
  157.7 18.0 %all-to-all-start.1 = ((f32[2,64,16,128]{3,2,0,1:T(8,128)}), f32[2,64,16,128]{3,2,0,1:T(8,128)S(1)}, u32[]{:S(2)}, u32[]{:S(2)}) async-start(f32[2,64,16,128]{3,2,0,1:T(8,128)} %copy.54), calls=%async_computation.1 | async-start | bytes 2097152 | tf_op jit(solution)/shard_map/while/body/eval_jaxpr/all_to_all | solution.py:77
  184.1 1.2 copy-start.5
  184.2 3.7 %copy-start.1 = (f32[9,16,4096]{2,0,1:T(8,128)S(1)}, f32[9,16,4096]{2,0,1:T(8,128)}, u32[]{:S(2)}) copy-start(f32[9,16,4096]{2,0,1:T(8,128)} %get-tuple-element.361) | copy-start | bytes 7077892 | tf_op jit(solution)/shard_map/while
  187.8 6.4 %copy-start.6 = (f32[3,16,4096]{2,0,1:T(4,128)}, f32[3,16,4096]{2,0,1:T(4,128)S(1)}, u32[]{:S(2)}) copy-start(f32[3,16,4096]{2,0,1:T(4,128)S(1)} %convolution_add_fusion.4) | copy-start | bytes 2359300 | tf_op jit(solution)/shard_map/while
  187.8 8.4 %copy-start.4 = (f32[3,16,4096]{2,1,0:T(8,128)S(1)}, f32[3,16,4096]{2,1,0:T(8,128)}, u32[]{:S(2)}) copy-start(f32[3,16,4096]{2,1,0:T(8,128)} %get-tuple-element.406) | copy-start | bytes 2359300 | tf_op jit(solution)/shard_map/while
  194.3 1.9 copy-start.2
  226.0 1.0 copy-start.8
  233.1 18.0 %all-to-all-start.1 = ((f32[2,64,16,128]{3,2,0,1:T(8,128)}), f32[2,64,16,128]{3,2,0,1:T(8,128)S(1)}, u32[]{:S(2)}, u32[]{:S(2)}) async-start(f32[2,64,16,128]{3,2,0,1:T(8,128)} %copy.54), calls=%async_computation.1 | async-start | bytes 2097152 | tf_op jit(solution)/shard_map/while/body/eval_jaxpr/all_to_all | solution.py:77
  259.6 1.2 copy-start.5
  259.6 3.7 %copy-start.1 = (f32[9,16,4096]{2,0,1:T(8,128)S(1)}, f32[9,16,4096]{2,0,1:T(8,128)}, u32[]{:S(2)}) copy-start(f32[9,16,4096]{2,0,1:T(8,128)} %get-tuple-element.361) | copy-start | bytes 7077892 | tf_op jit(solution)/shard_map/while
  263.3 6.4 %copy-start.6 = (f32[3,16,4096]{2,0,1:T(4,128)}, f32[3,16,4096]{2,0,1:T(4,128)S(1)}, u32[]{:S(2)}) copy-start(f32[3,16,4096]{2,0,1:T(4,128)S(1)} %convolution_add_fusion.4) | copy-start | bytes 2359300 | tf_op jit(solution)/shard_map/while
  263.3 8.4 %copy-start.4 = (f32[3,16,4096]{2,1,0:T(8,128)S(1)}, f32[3,16,4096]{2,1,0:T(8,128)}, u32[]{:S(2)}) copy-start(f32[3,16,4096]{2,1,0:T(8,128)} %get-tuple-element.406) | copy-start | bytes 2359300 | tf_op jit(solution)/shard_map/while
  269.7 1.9 copy-start.2
  275.2 42.0 %copy-start.7 = (f32[3,16,4096]{2,0,1:T(4,128)S(1)}, f32[3,16,4096]{2,0,1:T(4,128)}, u32[]{:S(2)}) copy-start(f32[3,16,4096]{2,0,1:T(4,128)} %get-tuple-element.393) | copy-start | bytes 2359300
  275.3 24.2 %collective-permute-start.3 = (f32[3,16,4096]{2,1,0:T(8,128)S(1)}, f32[3,16,4096]{2,1,0:T(8,128)S(1)}, u32[]{:S(2)}, u32[]{:S(2)}) collective-permute-start(f32[3,16,4096]{2,1,0:T(8,128)S(1)} %get-tuple-element.227), channel_id=1, source_target_pairs={{120,0},{124,4},{0,8},{4,12},{8,16},{12,20},{16,24},{20,28},{24,32... | collective-permute-start | bytes 2359304 | tf_op jit(solution)/shard_map/ppermute | solution.py:25
  275.4 41.8 %collective-permute-start.2 = (f32[3,16,4096]{2,1,0:T(8,128)S(1)}, f32[3,16,4096]{2,1,0:T(8,128)S(1)}, u32[]{:S(2)}, u32[]{:S(2)}) collective-permute-start(f32[3,16,4096]{2,1,0:T(8,128)S(1)} %get-tuple-element.226), channel_id=1, source_target_pairs={{124,0},{0,4},{4,8},{8,12},{12,16},{16,20},{20,24},{24,28},{28,32}... | collective-permute-start | bytes 2359304 | tf_op jit(solution)/shard_map/ppermute | solution.py:25
where the time goes:
time: 320 us; the launch traced here: 319 us
  waiting for transfers between devices  104 us (32%)
  matrix products  64 us (20%)
  local copies, waits for them, and re-layouts  59.6 us (19%)
  blocking collectives  50.9 us (16%)
  starting transfers between devices  25.1 us (8%)
  other arithmetic  14.3 us (4%)
    ppermute x4, waiting for transfers between devices, shifted(): return lax.ppermute(block, axis, route)  63.5 us
    all_to_all x3, blocking collectives, solve_poisson(): lax.all_to_all(spectrum, 'grid', split_axis=2, concat_axis=1, tiled=True)  50.9 us
    all_to_all x3, waiting for transfers between devices, solve_poisson(): lax.all_to_all(columns, 'grid', split_axis=1, concat_axis=2, tiled=True)  40.4 us
    dot_general x3, matrix products, one_turn(): jnp.einsum('sq,swt->qwt', visit_onehot_mask, weighted_density * leading_o...  19.2 us
    dot_general x12, matrix products, transform_axis(): jnp.einsum(formula, cosine_table, values_in, precision=EXACT_PRECISION)  17.1 us
    dot_general x12, matrix products, transform_axis(): jnp.einsum(formula, sine_table, values_in, precision=EXACT_PRECISION)  14.2 us
    all_to_all x3, starting transfers between devices, solve_poisson(): lax.all_to_all(columns, 'grid', split_axis=1, concat_axis=2, tiled=True)  13.6 us
    ppermute x4, starting transfers between devices, shifted(): return lax.ppermute(block, axis, route)  11.5 us
  transfers between devices with their start and end apart: 7, of which 7 were waited for; matrix products, arithmetic and copies ran while one was open for 3% of the time, Pallas kernels for 0%

commit v1 on v0

v1 whole, which is shorter than its diff:
```python
import functools

import jax
import jax.numpy as jnp
import numpy as np
from jax import lax
from jax.experimental import pallas as pl
from jax.experimental.pallas import tpu as pltpu
from jax.sharding import PartitionSpec as P

NG = 64
ORB = 3
MIXING = 0.25
BOX = 16.0
NC = 4
CY = 32 // NC
CL = CY * 128
PITCH = 72
MESH = pl.DeviceIdType.MESH
F32 = jnp.float32
BF16 = jnp.bfloat16


def hi_lo(values):
    hi = values.astype(BF16)
    return hi, (values - hi.astype(F32)).astype(BF16)


def host_hi_lo(values):
    hi = values.astype(np.float32).astype(BF16)
    return hi, (values - hi.astype(np.float64)).astype(np.float32).astype(BF16)


def tables():
    n = np.arange(NG)
    angle = 2.0 * np.pi * ((n[:, None] * n[None, :]) % NG) / NG
    h = (np.cos(angle) + np.sin(angle)) / 8.0
    hh, hl = host_hi_lo(h)
    ax = np.concatenate([hh, hl, hh], axis=1)
    bh, bl = host_hi_lo(np.kron(np.eye(2), h))
    wz = np.block([[bh, bl], [bh, np.zeros_like(bl)]])
    order = np.array([2 * (c % 32) + c // 32 for c in range(NG)])
    fh, fl = host_hi_lo(h[:, order])
    ay = np.concatenate([fh, fl, fh], axis=1)
    gh, gl = host_hi_lo(h[order, :])
    ai = np.concatenate([gh, gl, gh], axis=1)
    return ax, wz, ay, ai


def candidates():
    rows = []
    for first, second, same, kind in (
        (0, 2, False, 0),
        (1, 2, False, 1),
        (0, 1, False, 2),
        (1, 1, True, 3),
        (0, 0, True, 4),
        (2, 2, True, 5),
    ):
        for a in range(ORB):
            for b in range(ORB):
                if not same or a <= b:
                    rows.append((first, a, second, b, kind, 1))
    table = np.zeros((8, 128), np.int32)
    for c, row in enumerate(rows):
        table[:6, c] = row
    kind = np.where(table[5] > 0, table[4], -1)
    before = np.arange(128)[:, None] < np.arange(128)[None, :]
    same_kind = before & (kind[:, None] == kind[None, :])
    return table, same_kind.astype(np.float32), before.astype(np.float32)


def plan_kernel(slots, capacity, mask_ref, cand_ref, same_ref, before_ref, tab_ref, coef_ref):
    norb = mask_ref.shape[0]
    groups = norb // ORB
    group = lax.axis_index("band")
    m = mask_ref[...].astype(F32)
    rows = lax.broadcasted_iota(jnp.int32, (norb, norb), 0)
    cols = lax.broadcasted_iota(jnp.int32, (norb, norb), 1)
    brow = (rows * 21846) >> 16
    bcol = (cols * 21846) >> 16
    sep = jnp.where(bcol >= brow, bcol - brow, bcol - brow + groups)

    def row_sum(keep):
        return jnp.sum(jnp.where(keep, m, 0.0), axis=1, keepdims=True)

    r0 = row_sum((sep == 0) & (rows <= cols))
    r1 = row_sum(sep == 1)
    r2 = row_sum(sep == 2)
    gb = (lax.broadcasted_iota(jnp.int32, (norb, 128), 0) * 21846) >> 16
    lane = lax.broadcasted_iota(jnp.int32, (norb, 128), 1)
    nxt = jnp.where(gb == groups - 1, 0, gb + 1)
    prv = jnp.where(gb == 0, groups - 1, gb - 1)

    def to_lanes(values, place):
        return jnp.sum(jnp.where(place == lane, values, 0.0), axis=0, keepdims=True)

    n0 = to_lanes(r0, gb)
    n0_next = to_lanes(r0, prv)
    n1 = to_lanes(r1, gb)
    load = to_lanes(r2, nxt) + n1 + n0
    sub = lax.broadcasted_iota(jnp.int32, (128, 128), 0)
    lan = lax.broadcasted_iota(jnp.int32, (128, 128), 1)
    eye = sub == lan

    def to_rows(values):
        return jnp.sum(jnp.where(eye, values, 0.0), axis=1, keepdims=True)

    excess = jnp.where(sub < groups, to_rows(load) - capacity, 0.0)
    prefix = jnp.sum(jnp.where(sub <= lan, excess, 0.0), axis=0, keepdims=True)
    total = jnp.sum(excess, axis=0, keepdims=True)
    low = -jnp.floor(n0_next * 0.5)
    path = to_rows(prefix) - prefix + jnp.where(sub < lan, total, 0.0) + low
    flow = jnp.max(jnp.where(lan < groups, path, -1e9), axis=1, keepdims=True)

    left = jnp.where(group == 0, groups - 1, group - 1)
    right = jnp.where(group == groups - 1, 0, group + 1)
    sub1 = lax.broadcasted_iota(jnp.int32, (128, 1), 0)
    lan1 = lax.broadcasted_iota(jnp.int32, (1, 128), 1)

    def at_row(values, index):
        return jnp.sum(jnp.where(sub1 == index, values, 0.0), axis=0, keepdims=True)

    def at_lane(values, index):
        return jnp.sum(jnp.where(lan1 == index, values, 0.0), axis=1, keepdims=True)

    f_here, f_left = at_row(flow, group), at_row(flow, left)
    n1_here, n1_left = at_lane(n1, group), at_lane(n1, left)
    n0_here, n0_right = at_lane(n0, group), at_lane(n0, right)

    cand = cand_ref[...]

    def orbital_of(block, inner):
        b = group + block - 1
        b = jnp.where(b < 0, b + groups, jnp.where(b >= groups, b - groups, b))
        return b * ORB + inner

    row_id = orbital_of(cand[0:1], cand[1:2])
    col_id = orbital_of(cand[2:3], cand[3:4])
    kind = cand[4:5]
    valid = cand[5:6] > 0
    orb = lax.broadcasted_iota(jnp.int32, (norb, 128), 0)
    col_hot = (orb == col_id).astype(F32)
    picked = jnp.dot(m, col_hot, preferred_element_type=F32)
    live = jnp.sum(jnp.where(orb == row_id, picked, 0.0), axis=0, keepdims=True)
    live = jnp.where(valid, live, 0.0)
    rank = jnp.dot(
        jnp.broadcast_to(live, (8, 128)), same_ref[...], preferred_element_type=F32
    )[0:1]
    big = 1e9
    x1 = jnp.minimum(jnp.maximum(f_here, 0.0), n1_here)
    y1 = jnp.minimum(jnp.maximum(f_left, 0.0), n1_left)
    b0 = jnp.maximum(f_here - n1_here, 0.0)
    a0 = jnp.maximum(-f_left, 0.0)
    low_rank = jnp.where(
        kind == 1,
        x1,
        jnp.where(kind == 3, b0, jnp.where(kind == 5, n0_right - jnp.maximum(-f_here, 0.0), 0.0)),
    )
    high_rank = jnp.where(
        kind == 2,
        y1,
        jnp.where(
            kind == 3, n0_here - a0, jnp.where(kind == 4, jnp.maximum(f_left - n1_left, 0.0), big)
        ),
    )
    active = jnp.where((rank >= low_rank) & (rank < high_rank), live, 0.0)
    place = jnp.dot(
        jnp.broadcast_to(active, (8, 128)), before_ref[...], preferred_element_type=F32
    )[0:1]
    slot = lax.broadcasted_iota(jnp.int32, (slots, 128), 0).astype(F32)
    hot = jnp.where(place == slot, active, 0.0)
    first = (cand[0:1] * ORB + cand[1:2]).astype(F32)
    second = (cand[2:3] * ORB + cand[3:4]).astype(F32)
    i_of = jnp.sum(hot * first, axis=1, keepdims=True)
    j_of = jnp.sum(hot * second, axis=1, keepdims=True)
    w_of = jnp.sum(hot, axis=1, keepdims=True)
    lane_s = lax.broadcasted_iota(jnp.int32, (slots, 128), 1)
    tab_ref[...] = jnp.where(lane_s == 0, i_of, jnp.where(lane_s == 1, j_of, 0.0)).astype(jnp.int32)
    w_cross = jnp.where(i_of == j_of, 0.0, w_of)
    for q in range(3 * ORB):
        coef_ref[0, q] = jnp.broadcast_to(jnp.where(i_of == q, w_of, 0.0), (slots, 128))
        coef_ref[1, q] = jnp.broadcast_to(jnp.where(j_of == q, w_cross, 0.0), (slots, 128))


def plan(slots, capacity, pair_mask):
    table, same_kind, before = candidates()
    vmem = pl.BlockSpec(memory_space=pltpu.VMEM)
    return pl.pallas_call(
        functools.partial(plan_kernel, slots, float(capacity)),
        out_shape=(
            jax.ShapeDtypeStruct((slots, 128), jnp.int32),
            jax.ShapeDtypeStruct((2, 3 * ORB, slots, 128), F32),
        ),
        in_specs=[vmem] * 4,
        out_specs=(vmem, vmem),
        name="plan",
    )(pair_mask, jnp.asarray(table), jnp.asarray(same_kind), jnp.asarray(before))


def split_sum(low_mask, tall):
    half = tall.shape[0] // 2
    outs = []
    for t in range(tall.shape[1] // 128):
        top = tall[:half, t * 128 : (t + 1) * 128]
        bot = tall[half:, t * 128 : (t + 1) * 128]
        outs.append(
            jnp.where(low_mask, top, bot) + pltpu.roll(jnp.where(low_mask, bot, top), 64, 1)
        )
    return outs


def mega_kernel(rounds, *refs):
    (tab, coef, ax_ref, wz_ref, ay_ref, ai_ref, orb_hbm, out_ref) = refs[:8]
    orbs = refs[8 : 8 + NC]
    sums = refs[8 + NC : 8 + 2 * NC]
    back = refs[8 + 2 * NC : 8 + 3 * NC]
    (rho, cube, work, vout, vrecv, ktab) = refs[8 + 3 * NC : 14 + 3 * NC]
    (lsem, z1s, z1r, x1s, x1r, x2s, x2r, z2s, z2r) = refs[14 + 3 * NC :]

    groups = lax.axis_size("band")
    band = lax.axis_index("band")
    me = lax.axis_index("grid")
    left = lax.rem(band + groups - 1, groups)
    right = lax.rem(band + 1, groups)
    peers = {
        0: me,
        1: me + 1 - 2 * lax.rem(me, 2),
        2: lax.rem(me + 2, 4),
        3: 3 - me,
    }

    def local_copy(c):
        return pltpu.make_async_copy(
            orb_hbm.at[:, :, pl.ds(c * CL, CL)], orbs[c].at[pl.ds(ORB, ORB)], lsem.at[c]
        )

    for c in range(NC):
        local_copy(c).start()

    barrier = pltpu.get_barrier_semaphore()
    for target in (left, right):
        pl.semaphore_signal(barrier, inc=1, device_id=(target, me), device_id_type=MESH)
    for k in (1, 2, 3):
        pl.semaphore_signal(barrier, inc=1, device_id=(band, peers[k]), device_id_type=MESH)
    pl.semaphore_wait(barrier, 5)

    def z1(side, c):
        return pltpu.make_async_remote_copy(
            src_ref=orbs[c].at[pl.ds(ORB, ORB)],
            dst_ref=orbs[c].at[pl.ds(2 * ORB if side == 0 else 0, ORB)],
            send_sem=z1s.at[side, c],
            recv_sem=z1r.at[side, c],
            device_id=(left if side == 0 else right, me),
            device_id_type=MESH,
        )

    for c in range(NC):
        local_copy(c).wait()
        z1(0, c).start()
        z1(1, c).start()

    low_mask = lax.broadcasted_iota(jnp.int32, (32, 128), 1) < 64

    def signed(k):
        return jnp.where(k < NG // 2, k, k - NG)

    lane = lax.broadcasted_iota(jnp.int32, (32, 128), 1)
    sub = lax.broadcasted_iota(jnp.int32, (32, 128), 0)
    fy = signed(sub + jnp.where(low_mask, 0, 32))
    fz = signed(jnp.where(low_mask, lane, lane - 64))
    flat = fy * fy + fz * fz

    def fill(kx, carry):
        fx = signed(kx)
        squared = flat + fx * fx
        safe = jnp.maximum(squared, 1).astype(F32)
        ktab[pl.ds(pl.multiple_of(kx * 32, 32), 32), :] = jnp.where(
            squared > 0, (BOX * BOX / np.pi) / safe, 0.0
        )
        return carry

    lax.fori_loop(0, NG, fill, 0)

    def x1(k, r, c):
        return pltpu.make_async_remote_copy(
            src_ref=rho.at[k - 1, r, pl.ds(c * CY, CY)],
            dst_ref=cube.at[r, pl.ds(c * CY, CY), me],
            send_sem=x1s.at[k - 1, r, c],
            recv_sem=x1r.at[k - 1, r, c],
            device_id=(band, peers[k]),
            device_id_type=MESH,
        )

    def x2(k, r, c):
        return pltpu.make_async_remote_copy(
            src_ref=vout.at[r, pl.ds(c * CY, CY), peers[k]],
            dst_ref=vrecv.at[k - 1, r, pl.ds(c * CY, CY)],
            send_sem=x2s.at[k - 1, r, c],
            recv_sem=x2r.at[k - 1, r, c],
            device_id=(band, peers[k]),
            device_id_type=MESH,
        )

    def z2(side, c):
        return pltpu.make_async_remote_copy(
            src_ref=sums[c].at[pl.ds(0 if side == 0 else 2 * ORB, ORB)],
            dst_ref=back[c].at[1 if side == 0 else 0],
            send_sem=z2s.at[side, c],
            recv_sem=z2r.at[side, c],
            device_id=(left if side == 0 else right, me),
            device_id_type=MESH,
        )

    def lanes(y):
        return pl.ds(pl.multiple_of(y * 128, 128), 128)

    for c in range(NC):
        z1(0, c).wait_recv()
        z1(1, c).wait_recv()
        for r in range(rounds):
            ids = {}
            for k in (2, 3, 1, 0):
                slot = r * 4 + peers[k]
                ids[k] = (tab[slot, 0], tab[slot, 1])

            def densities(y, carry, c=c, r=r, ids=ids):
                for k in (2, 3, 1, 0):
                    i, j = ids[k]
                    value = orbs[c][i, :, lanes(y)] * orbs[c][j, :, lanes(y)]
                    if k == 0:
                        cube[r, c * CY + y, me] = value
                    else:
                        rho[k - 1, r, c * CY + y] = value
                return carry

            lax.fori_loop(0, CY, densities, 0)
            for k in (2, 3, 1):
                x1(k, r, c).start()

    ax = ax_ref[...]
    wz = wz_ref[...]

    def along_z(tiles):
        stacked = jnp.concatenate(tiles, axis=0)
        hi, lo = hi_lo(stacked)
        wide = jnp.dot(jnp.concatenate([hi, lo], axis=1), wz, preferred_element_type=F32)
        both = wide[:, :128] + wide[:, 128:]
        return [both[t * NG : (t + 1) * NG] for t in range(len(tiles))]

    def along_x(tiles):
        outs = []
        for t in range(0, len(tiles), 2):
            hi, lo = hi_lo(jnp.concatenate([tiles[t], tiles[t + 1]], axis=1))
            wide = jnp.dot(ax, jnp.concatenate([hi, hi, lo], axis=0), preferred_element_type=F32)
            outs += [wide[:, :128], wide[:, 128:]]
        return outs

    def work_rows(r, y):
        return pl.ds(pl.multiple_of((r * 32 + y) * PITCH, 8), NG)

    def forward(step, carry):
        c, r = step // rounds, lax.rem(step, rounds)
        for k in (1, 2, 3):
            x1(k, r, c).wait_recv()
        tiles = [cube[r, c * CY + t].reshape(NG, 128) for t in range(CY)]
        tiles = along_z(along_x(tiles))
        for t in range(CY):
            work[work_rows(r, c * CY + t), :] = tiles[t]
        return carry

    lax.fori_loop(0, NC * rounds, forward, 0)

    def spread(tiles):
        hi, lo = hi_lo(jnp.concatenate(tiles, axis=1))
        mask = lax.rem(lax.broadcasted_iota(jnp.int32, hi.shape, 1), 128) < 64
        zero = jnp.zeros_like(hi)
        h0, h1 = jnp.where(mask, hi, zero), jnp.where(mask, zero, hi)
        l0, l1 = jnp.where(mask, lo, zero), jnp.where(mask, zero, lo)
        return jnp.concatenate([h0, h1, h0, h1, l0, l1], axis=0)

    ay = ay_ref[...]
    ai = ai_ref[...]
    KX = 8

    def middle(step, carry):
        r, g = step // (NG // KX), lax.rem(step, NG // KX)
        base = r * (32 * PITCH) + g * KX
        for t in range(0, KX, 2):
            tiles = [work[pl.ds(base + t + u, 32, stride=PITCH), :] for u in range(2)]
            tiles = split_sum(low_mask, jnp.dot(ay, spread(tiles), preferred_element_type=F32))
            tiles = [
                tiles[u] * ktab[pl.ds(pl.multiple_of((g * KX + t + u) * 32, 32), 32), :]
                for u in range(2)
            ]
            tiles = split_sum(low_mask, jnp.dot(ai, spread(tiles), preferred_element_type=F32))
            for u in range(2):
                work[pl.ds(base + t + u, 32, stride=PITCH), :] = tiles[u]
        return carry

    lax.fori_loop(0, rounds * (NG // KX), middle, 0)

    def inverse(step, carry):
        c, r = step // rounds, lax.rem(step, rounds)
        tiles = [work[work_rows(r, c * CY + t), :] for t in range(CY)]
        tiles = along_x(along_z(tiles))
        for t in range(CY):
            vout[r, c * CY + t] = tiles[t].reshape(4, 16, 128)
        for k in (2, 3, 1):
            x2(k, r, c).start()
        return carry

    lax.fori_loop(0, NC * rounds, inverse, 0)

    for c in range(NC):
        for r in range(rounds):
            for k in (1, 2, 3):
                x2(k, r, c).wait_recv()
        ids = {}
        for r in range(rounds):
            for k in range(4):
                slot = r * 4 + peers[k]
                ids[r, k] = (slot, tab[slot, 0], tab[slot, 1])

        def accumulate(y, carry, c=c, ids=ids):
            totals = [jnp.zeros((16, 128), F32) for _ in range(3 * ORB)]
            for r in range(rounds):
                for k in range(4):
                    slot, i, j = ids[r, k]
                    if k == 0:
                        v = vout[r, c * CY + y, me]
                    else:
                        v = vrecv[k - 1, r, c * CY + y]
                    on_i = v * orbs[c][j, :, lanes(y)]
                    on_j = v * orbs[c][i, :, lanes(y)]
                    for q in range(3 * ORB):
                        totals[q] = (
                            totals[q]
                            + coef[0, q, pl.ds(slot, 1), :] * on_i
                            + coef[1, q, pl.ds(slot, 1), :] * on_j
                        )
            for q in range(3 * ORB):
                sums[c][q, :, lanes(y)] = totals[q]
            return carry

        lax.fori_loop(0, CY, accumulate, 0)
        z2(0, c).start()
        z2(1, c).start()

    for c in range(NC):
        z2(0, c).wait_recv()
        z2(1, c).wait_recv()
        for a in range(ORB):
            out_ref[a, :, pl.ds(c * CL, CL)] = -MIXING * (
                sums[c][ORB + a] + (back[c][0, a] + back[c][1, a])
            )

    for c in range(NC):
        for side in range(2):
            z1(side, c).wait_send()
            z2(side, c).wait_send()

    def drain(step, carry):
        c, r = step // rounds, lax.rem(step, rounds)
        for k in (1, 2, 3):
            x1(k, r, c).wait_send()
            x2(k, r, c).wait_send()
        return carry

    lax.fori_loop(0, NC * rounds, drain, 0)


def mega(rounds, collective_id, tab, coef, orbitals):
    ax, wz, ay, ai = tables()
    vmem = pl.BlockSpec(memory_space=pltpu.VMEM)
    planes = orbitals.shape[1]
    dma = pltpu.SemaphoreType.DMA
    return pl.pallas_call(
        functools.partial(mega_kernel, rounds),
        out_shape=jax.ShapeDtypeStruct(orbitals.shape, F32),
        in_specs=[pl.BlockSpec(memory_space=pltpu.SMEM)]
        + [vmem] * 5
        + [pl.BlockSpec(memory_space=pl.ANY)],
        out_specs=vmem,
        scratch_shapes=[pltpu.VMEM((3 * ORB, planes, CL), F32) for _ in range(2 * NC)]
        + [pltpu.VMEM((2, ORB, planes, CL), F32) for _ in range(NC)]
        + [
            pltpu.VMEM((3, rounds, 32, planes, 128), F32),
            pltpu.VMEM((rounds, 32, 4, planes, 128), F32),
            pltpu.VMEM((rounds * 32 * PITCH, 128), F32),
            pltpu.VMEM((rounds, 32, 4, planes, 128), F32),
            pltpu.VMEM((3, rounds, 32, planes, 128), F32),
            pltpu.VMEM((NG * 32, 128), F32),
            dma((NC,)),
            dma((2, NC)),
            dma((2, NC)),
            dma((3, rounds, NC)),
            dma((3, rounds, NC)),
            dma((3, rounds, NC)),
            dma((3, rounds, NC)),
            dma((2, NC)),
            dma((2, NC)),
        ],
        compiler_params=pltpu.CompilerParams(
            collective_id=collective_id, has_side_effects=True, vmem_limit_bytes=56 * 1024 * 1024
        ),
        name="mega%d" % rounds,
    )(
        tab,
        coef,
        jnp.asarray(ax),
        jnp.asarray(wz),
        jnp.asarray(ay),
        jnp.asarray(ai),
        orbitals,
    )


def local(orbitals, pair_mask):
    tab, coef = plan(16, 12, pair_mask)
    return mega(3, 3, tab, coef, orbitals)


def solution(mesh):
    return jax.shard_map(
        local,
        mesh=mesh,
        in_specs=(P("band", "grid", None), P()),
        out_specs=P("band", "grid", None),
        check_vma=False,
    )
```

time: 320 us -> 137 us (0.43)
  Pallas kernels: 0 us -> 135 us
  waiting for transfers between devices: 104 us -> 0 us
  matrix products: 64 us -> 0 us
  local copies, waits for them, and re-layouts: 59.6 us -> 2.06 us
  blocking collectives: 50.9 us -> 0 us
  starting transfers between devices: 25.1 us -> 0 us
  other arithmetic: 14.3 us -> 0 us
    pallas_call x0 -> x2, Pallas kernels: none -> 135 us  [the longest x1 132 us: mega(): pl.pallas_call(functools.partial(mega_kernel, rounds), out_shape=jax.Shap...]
    dot_general x36 -> x0, matrix products: 64 us -> none  [the longest x3 19.2 us: one_turn(): jnp.einsum('sq,swt->qwt', visit_onehot_mask, weighted_density * leading_o...]
    ppermute x4 -> x0, waiting for transfers between devices: 63.5 us -> none  [shifted(): return lax.ppermute(block, axis, route)]
    all_to_all x3 -> x0, blocking collectives: 50.9 us -> none  [solve_poisson(): lax.all_to_all(spectrum, 'grid', split_axis=2, concat_axis=1, tiled=True)]
    all_to_all x3 -> x0, waiting for transfers between devices: 40.4 us -> none  [solve_poisson(): lax.all_to_all(columns, 'grid', split_axis=1, concat_axis=2, tiled=True)]
    gather x12 -> x0, local copies, waits for them, and re-layouts: 14.2 us -> none  [the longest x3 6.84 us: one_turn(): second_orb = flat_visiting[slot_turn]]
    while x37 -> x0, local copies, waits for them, and re-layouts: 13.9 us -> none
    all_to_all x3 -> x0, starting transfers between devices: 13.6 us -> none  [solve_poisson(): lax.all_to_all(columns, 'grid', split_axis=1, concat_axis=2, tiled=True)]
  transfers between devices with their start and end apart: 7 -> 0, of which waited for: 7 -> 0; matrix products, arithmetic and copies ran while one was open for 3% -> 0% of each run, Pallas kernels for 0% -> 0%
where the time goes in v1:
time: 137 us
  Pallas kernels  135 us (99%)
  local copies, waits for them, and re-layouts  2.06 us (2%)
    pallas_call x1, Pallas kernels, mega(): pl.pallas_call(functools.partial(mega_kernel, rounds), out_shape=jax.Shap...  132 us

profile of v1, /device:TPU:1, one launch (start us, length us, event | category | flops | bytes accessed | tf_op | source)
XLA Modules:
  0.0 136.6 jit_solution(4814457776671231951)
XLA Ops:
  0.0 2.2 %plan.1 = (s32[16,128]{1,0:T(8,128)}, f32[2,9,16,128]{3,2,1,0:T(8,128)}) custom-call(s32[96,96]{1,0:T(8,128)} %mask_ref.1, s32[8,128]{1,0:T(8,128)} %constant.14.clone.cand_ref, f32[128,128]{1,0:T(8,128)} %constant.15.clone.same_ref, f32[128,128]{1,0:T(8,128)} %constant.16.clone.before_ref), custom_call_target="tpu_custom_call" | custom-call | tf_op jit(solution)/shard_map/plan/pallas_call | solution.py:189
  2.2 132.3 %mega3.1 = f32[3,16,4096]{2,1,0:T(8,128)} custom-call(s32[16,128]{1,0:T(8,128)} %get-tuple-element.7.refs_0_, f32[2,9,16,128]{3,2,1,0:T(8,128)} %get-tuple-element.8.refs_1_, bf16[64,192]{1,0:T(8,128)(2,1)} %constant.17.clone.refs_2_, bf16[256,256]{1,0:T(8,128)(2,1)} %constant.18.clone.refs_3_, bf16[64,192]{1,0:T(8,128)(2,1)} %constant.19.clone.refs_4_, ...), custom_call_target="tpu_custom_call" | custom-call | tf_op jit(solution)/shard_map/mega3/pallas_call | solution.py:478
  134.5 2.1 %copy.11 = f32[3,16,4096]{2,1,0:T(8,128)} copy(f32[3,16,4096]{2,1,0:T(8,128)} %mega3.1) | data formatting | bytes 1572864

commit v2 on v1

--- a/solution.py
+++ b/solution.py
@@ -15,6 +15,8 @@
 NC = 4
 CY = 32 // NC
 CL = CY * 128
+KX = 16
+CLASSES = ((8, 12), (10, 12), (12, 12))
 PITCH = 72
 MESH = pl.DeviceIdType.MESH
 F32 = jnp.float32
@@ -39,10 +41,10 @@
     ax = np.concatenate([hh, hl, hh], axis=1)
     bh, bl = host_hi_lo(np.kron(np.eye(2), h))
     wz = np.block([[bh, bl], [bh, np.zeros_like(bl)]])
-    order = np.array([2 * (c % 32) + c // 32 for c in range(NG)])
-    fh, fl = host_hi_lo(h[:, order])
+    fh, fl = host_hi_lo(np.concatenate([h[:, 0::2], h[:, 1::2]], axis=0))
     ay = np.concatenate([fh, fl, fh], axis=1)
-    gh, gl = host_hi_lo(h[order, :])
+    back = np.concatenate([h[0::2], h[1::2]], axis=0)
+    gh, gl = host_hi_lo(np.concatenate([back[:, :32], back[:, 32:]], axis=0))
     ai = np.concatenate([gh, gl, gh], axis=1)
     return ax, wz, ay, ai
 
@@ -70,7 +72,7 @@
     return table, same_kind.astype(np.float32), before.astype(np.float32)
 
 
-def plan_kernel(slots, capacity, mask_ref, cand_ref, same_ref, before_ref, tab_ref, coef_ref):
+def plan_kernel(slots, classes, mask_ref, cand_ref, same_ref, before_ref, tab_ref, coef_ref, class_ref):
     norb = mask_ref.shape[0]
     groups = norb // ORB
     group = lax.axis_index("band")
@@ -106,12 +108,28 @@
     def to_rows(values):
         return jnp.sum(jnp.where(eye, values, 0.0), axis=1, keepdims=True)
 
-    excess = jnp.where(sub < groups, to_rows(load) - capacity, 0.0)
-    prefix = jnp.sum(jnp.where(sub <= lan, excess, 0.0), axis=0, keepdims=True)
-    total = jnp.sum(excess, axis=0, keepdims=True)
     low = -jnp.floor(n0_next * 0.5)
-    path = to_rows(prefix) - prefix + jnp.where(sub < lan, total, 0.0) + low
-    flow = jnp.max(jnp.where(lan < groups, path, -1e9), axis=1, keepdims=True)
+    high = to_rows(n1 + jnp.floor((n0 + 1.0) * 0.5))
+    load_rows = to_rows(load)
+    is_edge = lax.rem((sub + 1) // 2, 2) == 0
+    choice, flow = None, None
+    for index in reversed(range(len(classes))):
+        edge, inner = classes[index]
+        excess = load_rows - jnp.where(is_edge, float(edge), float(inner))
+        excess = jnp.where(sub < groups, excess, 0.0)
+        prefix = jnp.sum(jnp.where(sub <= lan, excess, 0.0), axis=0, keepdims=True)
+        total = jnp.sum(excess, axis=0, keepdims=True)
+        path = to_rows(prefix) - prefix + jnp.where(sub < lan, total, 0.0) + low
+        need = jnp.max(jnp.where(lan < groups, path, -1e9), axis=1, keepdims=True)
+        if choice is None:
+            choice, flow = jnp.full((1, 1), float(index), F32), need
+        else:
+            over = jnp.where(sub[:, :1] < groups, need - high, -1e9)
+            worst = jnp.maximum(jnp.max(over, axis=0, keepdims=True), total[:, :1])
+            fits = worst < 0.5
+            choice = jnp.where(fits, float(index), choice)
+            flow = jnp.where(fits, need, flow)
+    class_ref[...] = jnp.broadcast_to(choice, (8, 128)).astype(jnp.int32)
 
     left = jnp.where(group == 0, groups - 1, group - 1)
     right = jnp.where(group == groups - 1, 0, group + 1)
@@ -183,34 +201,36 @@
         coef_ref[1, q] = jnp.broadcast_to(jnp.where(j_of == q, w_cross, 0.0), (slots, 128))
 
 
-def plan(slots, capacity, pair_mask):
+def plan(slots, classes, pair_mask):
     table, same_kind, before = candidates()
     vmem = pl.BlockSpec(memory_space=pltpu.VMEM)
     return pl.pallas_call(
-        functools.partial(plan_kernel, slots, float(capacity)),
+        functools.partial(plan_kernel, slots, classes),
         out_shape=(
             jax.ShapeDtypeStruct((slots, 128), jnp.int32),
             jax.ShapeDtypeStruct((2, 3 * ORB, slots, 128), F32),
+            jax.ShapeDtypeStruct((8, 128), jnp.int32),
         ),
         in_specs=[vmem] * 4,
-        out_specs=(vmem, vmem),
+        out_specs=(vmem, vmem, vmem),
         name="plan",
     )(pair_mask, jnp.asarray(table), jnp.asarray(same_kind), jnp.asarray(before))
 
 
 def split_sum(low_mask, tall):
-    half = tall.shape[0] // 2
     outs = []
     for t in range(tall.shape[1] // 128):
-        top = tall[:half, t * 128 : (t + 1) * 128]
-        bot = tall[half:, t * 128 : (t + 1) * 128]
+        top0, bot0, top1, bot1 = (
+            tall[32 * u : 32 * (u + 1), t * 128 : (t + 1) * 128] for u in range(4)
+        )
         outs.append(
-            jnp.where(low_mask, top, bot) + pltpu.roll(jnp.where(low_mask, bot, top), 64, 1)
+            jnp.where(low_mask, top0, bot1) + pltpu.roll(jnp.where(low_mask, bot0, top1), 64, 1)
         )
     return outs
 
 
-def mega_kernel(rounds, *refs):
+def mega_kernel(edge_slots, inner_slots, *refs):
+    rounds = (max(edge_slots, inner_slots) + 3) // 4
     (tab, coef, ax_ref, wz_ref, ay_ref, ai_ref, orb_hbm, out_ref) = refs[:8]
     orbs = refs[8 : 8 + NC]
     sums = refs[8 + NC : 8 + 2 * NC]
@@ -221,6 +241,11 @@
     groups = lax.axis_size("band")
     band = lax.axis_index("band")
     me = lax.axis_index("grid")
+    on_edge = 1 - lax.rem((lax.rem(band, 4) + 1) // 2, 2)
+    halves = inner_slots // 2 + on_edge * (edge_slots // 2 - inner_slots // 2)
+    chip, core = me // 2, lax.rem(me, 2)
+    mine = (halves - core + 1) // 2
+    others = (halves + core) // 2
     left = lax.rem(band + groups - 1, groups)
     right = lax.rem(band + 1, groups)
     peers = {
@@ -315,28 +340,48 @@
     def lanes(y):
         return pl.ds(pl.multiple_of(y * 128, 128), 128)
 
-    for c in range(NC):
-        z1(0, c).wait_recv()
-        z1(1, c).wait_recv()
-        for r in range(rounds):
-            ids = {}
-            for k in (2, 3, 1, 0):
-                slot = r * 4 + peers[k]
-                ids[k] = (tab[slot, 0], tab[slot, 1])
-
-            def densities(y, carry, c=c, r=r, ids=ids):
-                for k in (2, 3, 1, 0):
-                    i, j = ids[k]
-                    value = orbs[c][i, :, lanes(y)] * orbs[c][j, :, lanes(y)]
-                    if k == 0:
-                        cube[r, c * CY + y, me] = value
-                    else:
-                        rho[k - 1, r, c * CY + y] = value
-                return carry
-
-            lax.fori_loop(0, CY, densities, 0)
-            for k in (2, 3, 1):
+    def slot_of(k, r):
+        half = 2 * r + (core if k in (0, 2) else 1 - core)
+        return 2 * half + (chip if k in (0, 1) else 1 - chip)
+
+    def densities(c, r, targets):
+        ids = []
+        for k in targets:
+            slot = slot_of(k, r)
+            ids.append((k, tab[slot, 0], tab[slot, 1]))
+
+        def one_tile(y, carry):
+            for k, i, j in ids:
+                value = orbs[c][i, :, lanes(y)] * orbs[c][j, :, lanes(y)]
+                if k == 0:
+                    cube[r, c * CY + y, me] = value
+                else:
+                    rho[k - 1, r, c * CY + y] = value
+            return carry
+
+        lax.fori_loop(0, CY, one_tile, 0)
+        for k in targets:
+            if k:
                 x1(k, r, c).start()
+
+    order = [(0, 0), (0, 1), (1, 0), (2, 0), (1, 1), (3, 0), (2, 1), (3, 1)]
+    order += [(c, r) for r in range(2, rounds) for c in range(NC)]
+    seen = set()
+    for c, r in order:
+        if r >= rounds:
+            continue
+        if c not in seen:
+            seen.add(c)
+            z1(0, c).wait_recv()
+            z1(1, c).wait_recv()
+
+        @pl.when(r < mine)
+        def _():
+            densities(c, r, (2, 0))
+
+        @pl.when(r < others)
+        def _():
+            densities(c, r, (3, 1))
 
     ax = ax_ref[...]
     wz = wz_ref[...]
@@ -359,32 +404,22 @@
     def work_rows(r, y):
         return pl.ds(pl.multiple_of((r * 32 + y) * PITCH, 8), NG)
 
-    def forward(step, carry):
-        c, r = step // rounds, lax.rem(step, rounds)
+    def forward(r, c):
         for k in (1, 2, 3):
             x1(k, r, c).wait_recv()
         tiles = [cube[r, c * CY + t].reshape(NG, 128) for t in range(CY)]
         tiles = along_z(along_x(tiles))
         for t in range(CY):
             work[work_rows(r, c * CY + t), :] = tiles[t]
-        return carry
-
-    lax.fori_loop(0, NC * rounds, forward, 0)
 
     def spread(tiles):
         hi, lo = hi_lo(jnp.concatenate(tiles, axis=1))
-        mask = lax.rem(lax.broadcasted_iota(jnp.int32, hi.shape, 1), 128) < 64
-        zero = jnp.zeros_like(hi)
-        h0, h1 = jnp.where(mask, hi, zero), jnp.where(mask, zero, hi)
-        l0, l1 = jnp.where(mask, lo, zero), jnp.where(mask, zero, lo)
-        return jnp.concatenate([h0, h1, h0, h1, l0, l1], axis=0)
+        return jnp.concatenate([hi, hi, lo], axis=0)
 
     ay = ay_ref[...]
     ai = ai_ref[...]
-    KX = 8
-
-    def middle(step, carry):
-        r, g = step // (NG // KX), lax.rem(step, NG // KX)
+
+    def middle(r, g):
         base = r * (32 * PITCH) + g * KX
         for t in range(0, KX, 2):
             tiles = [work[pl.ds(base + t + u, 32, stride=PITCH), :] for u in range(2)]
@@ -396,54 +431,75 @@
             tiles = split_sum(low_mask, jnp.dot(ai, spread(tiles), preferred_element_type=F32))
             for u in range(2):
                 work[pl.ds(base + t + u, 32, stride=PITCH), :] = tiles[u]
-        return carry
-
-    lax.fori_loop(0, rounds * (NG // KX), middle, 0)
-
-    def inverse(step, carry):
-        c, r = step // rounds, lax.rem(step, rounds)
+
+    def inverse(r, c):
         tiles = [work[work_rows(r, c * CY + t), :] for t in range(CY)]
         tiles = along_x(along_z(tiles))
         for t in range(CY):
             vout[r, c * CY + t] = tiles[t].reshape(4, 16, 128)
         for k in (2, 3, 1):
             x2(k, r, c).start()
-        return carry
-
-    lax.fori_loop(0, NC * rounds, inverse, 0)
+
+    def looped(count, step):
+        def body(i, carry):
+            step(i)
+            return carry
+
+        lax.fori_loop(0, count, body, 0)
+
+    @functools.partial(looped, mine)
+    def _(r):
+        looped(NC, functools.partial(forward, r))
+        looped(NG // KX, functools.partial(middle, r))
+        looped(NC, functools.partial(inverse, r))
 
     for c in range(NC):
-        for r in range(rounds):
-            for k in (1, 2, 3):
+        sums[c][...] = jnp.zeros_like(sums[c])
+
+    def accumulate(c, r, sources):
+        ids = []
+        for k in sources:
+            slot = slot_of(k, r)
+            ids.append((k, slot, tab[slot, 0], tab[slot, 1]))
+            if k:
                 x2(k, r, c).wait_recv()
-        ids = {}
-        for r in range(rounds):
-            for k in range(4):
-                slot = r * 4 + peers[k]
-                ids[r, k] = (slot, tab[slot, 0], tab[slot, 1])
-
-        def accumulate(y, carry, c=c, ids=ids):
-            totals = [jnp.zeros((16, 128), F32) for _ in range(3 * ORB)]
-            for r in range(rounds):
-                for k in range(4):
-                    slot, i, j = ids[r, k]
-                    if k == 0:
-                        v = vout[r, c * CY + y, me]
-                    else:
-                        v = vrecv[k - 1, r, c * CY + y]
-                    on_i = v * orbs[c][j, :, lanes(y)]
-                    on_j = v * orbs[c][i, :, lanes(y)]
-                    for q in range(3 * ORB):
-                        totals[q] = (
-                            totals[q]
-                            + coef[0, q, pl.ds(slot, 1), :] * on_i
-                            + coef[1, q, pl.ds(slot, 1), :] * on_j
-                        )
+
+        @functools.partial(looped, CY)
+        def _(y):
+            totals = [sums[c][q, :, lanes(y)] for q in range(3 * ORB)]
+            for k, slot, i, j in ids:
+                if k == 0:
+                    v = vout[r, c * CY + y, me]
+                else:
+                    v = vrecv[k - 1, r, c * CY + y]
+                on_i = v * orbs[c][j, :, lanes(y)]
+                on_j = v * orbs[c][i, :, lanes(y)]
+                for q in range(3 * ORB):
+                    totals[q] = totals[q] + (
+                        coef[0, q, pl.ds(slot, 1), :] * on_i
+                        + coef[1, q, pl.ds(slot, 1), :] * on_j
+                    )
             for q in range(3 * ORB):
                 sums[c][q, :, lanes(y)] = totals[q]
-            return carry
-
-        lax.fori_loop(0, CY, accumulate, 0)
+
+    def both(c, r):
+        @pl.when(r < mine)
+        def _():
+            accumulate(c, r, (0, 2))
+
+        @pl.when(r < others)
+        def _():
+            accumulate(c, r, (1, 3))
+
+    last = (halves + 1) // 2 - 1
+
+    @functools.partial(looped, last)
+    def _(r):
+        for c in range(NC):
+            both(c, r)
+
+    for c in range(NC):
+        both(c, last)
         z2(0, c).start()
         z2(1, c).start()
 
@@ -460,23 +516,28 @@
             z1(side, c).wait_send()
             z2(side, c).wait_send()
 
-    def drain(step, carry):
-        c, r = step // rounds, lax.rem(step, rounds)
-        for k in (1, 2, 3):
-            x1(k, r, c).wait_send()
-            x2(k, r, c).wait_send()
-        return carry
-
-    lax.fori_loop(0, NC * rounds, drain, 0)
-
-
-def mega(rounds, collective_id, tab, coef, orbitals):
+    @functools.partial(looped, mine)
+    def _(r):
+        for c in range(NC):
+            x1(2, r, c).wait_send()
+            for k in (1, 2, 3):
+                x2(k, r, c).wait_send()
+
+    @functools.partial(looped, others)
+    def _(r):
+        for c in range(NC):
+            for k in (1, 3):
+                x1(k, r, c).wait_send()
+
+
+def mega(slots, collective_id, tab, coef, orbitals):
+    rounds = (max(slots) + 3) // 4
     ax, wz, ay, ai = tables()
     vmem = pl.BlockSpec(memory_space=pltpu.VMEM)
     planes = orbitals.shape[1]
     dma = pltpu.SemaphoreType.DMA
     return pl.pallas_call(
-        functools.partial(mega_kernel, rounds),
+        functools.partial(mega_kernel, *slots),
         out_shape=jax.ShapeDtypeStruct(orbitals.shape, F32),
         in_specs=[pl.BlockSpec(memory_space=pltpu.SMEM)]
         + [vmem] * 5
@@ -504,7 +565,7 @@
         compiler_params=pltpu.CompilerParams(
             collective_id=collective_id, has_side_effects=True, vmem_limit_bytes=56 * 1024 * 1024
         ),
-        name="mega%d" % rounds,
+        name="mega%d_%d" % slots,
     )(
         tab,
         coef,
@@ -517,8 +578,11 @@
 
 
 def local(orbitals, pair_mask):
-    tab, coef = plan(16, 12, pair_mask)
-    return mega(3, 3, tab, coef, orbitals)
+    tab, coef, index = plan(16, CLASSES, pair_mask)
+    branches = [functools.partial(mega, slots, 3 + n) for n, slots in enumerate(CLASSES)]
+    if len(branches) == 1:
+        return branches[0](tab, coef, orbitals)
+    return lax.switch(index[0, 0], branches, tab, coef, orbitals)
 
 
 def solution(mesh):

time: 137 us -> 106 us (0.77); the launches traced: 137 us -> 107 us
  Pallas kernels: 135 us -> 105 us
    pallas_call x2, Pallas kernels: 135 us -> 105 us  [the longest x1 103 us: mega(): pl.pallas_call(functools.partial(mega_kernel, *slots), out_shape=jax.Shap...]
where the time goes in v2:
time: 106 us; the launch traced here: 107 us
  Pallas kernels  105 us (99%)
  local copies, waits for them, and re-layouts  2.08 us (2%)
    pallas_call x1, Pallas kernels, mega(): pl.pallas_call(functools.partial(mega_kernel, *slots), out_shape=jax.Shap...  103 us

profile of v2, /device:TPU:1, one launch (start us, length us, event | category | flops | bytes accessed | tf_op | source)
XLA Modules:
  0.0 107.3 jit_solution(1801920553401278927)
XLA Ops:
  0.0 0.0 copy-start
  0.0 0.0 copy-start.1
  0.0 0.0 copy-start.2
  0.0 1.9 %plan.1 = (s32[16,128]{1,0:T(8,128)S(1)}, f32[2,9,16,128]{3,2,1,0:T(8,128)S(1)}, s32[8,128]{1,0:T(8,128)}) custom-call(s32[96,96]{1,0:T(8,128)} %mask_ref.1, s32[8,128]{1,0:T(8,128)} %constant.20.clone.cand_ref, f32[128,128]{1,0:T(8,128)} %constant.21.clone.same_ref, f32[128,128]{1,0:T(8,128)} %constant.22.clone.before_ref), custom_call_target="tpu_custom_call" | custom-call | tf_op jit(solution)/shard_map/plan/pallas_call | solution.py:207
  1.9 1.2 %slice.3 = s32[1,1]{1,0:T(1,128)} slice(s32[8,128]{1,0:T(8,128)} %get-tuple-element.75), slice={[0:1], [0:1]} | slice | bytes 8 | tf_op jit(solution)/shard_map/slice | solution.py:585
  3.7 0.0 copy-done
  3.7 0.0 copy-done.1
  3.7 0.0 copy-done.2
  3.7 102.6 %conditional.1 = (f32[3,16,4096]{2,1,0:T(8,128)S(1)}) conditional(s32[]{:T(128)} %bitcast, (s32[16,128]{1,0:T(8,128)S(1)}, f32[2,9,16,128]{3,2,1,0:T(8,128)S(1)}, bf16[64,192]{1,0:T(8,128)(2,1)}, bf16[256,256]{1,0:T(8,128)(2,1)S(1)}, bf16[128,96]{1,0:T(8,128)(2,1)S(1)}, /*index=5*/bf16[128,96]{1,0:T(8,128)(2,1)S(1)}, ...), branch_computations={%region_0.0_spmd, %region_1.0_spmd, %region_2.0_spmd} | conditional | bytes 8 | solution.py:585
  3.8 102.6 %mega10_12.1 = f32[3,16,4096]{2,1,0:T(8,128)S(1)} custom-call(s32[16,128]{1,0:T(8,128)S(1)} %get-tuple-element.58.refs_0_, f32[2,9,16,128]{3,2,1,0:T(8,128)S(1)} %get-tuple-element.59.refs_1_, bf16[64,192]{1,0:T(8,128)(2,1)} %get-tuple-element.60.refs_2_, bf16[256,256]{1,0:T(8,128)(2,1)S(1)} %get-tuple-element.61.refs_3_, ...), custom_call_target="tpu_custom_call" | custom-call | tf_op jit(solution)/shard_map/cond/branch_1_fun/mega10_12/pallas_call | solution.py:539
  106.4 0.9 copy.25
Async XLA Ops:
  0.0 3.7 %copy-start = (bf16[256,256]{1,0:T(8,128)(2,1)S(1)}, bf16[256,256]{1,0:T(8,128)(2,1)}, u32[]{:S(2)}) copy-start(bf16[256,256]{1,0:T(8,128)(2,1)} %constant.24.clone) | copy-start | bytes 393220
  0.0 3.7 %copy-start.1 = (bf16[128,96]{1,0:T(8,128)(2,1)S(1)}, bf16[128,96]{1,0:T(8,128)(2,1)}, u32[]{:S(2)}) copy-start(bf16[128,96]{1,0:T(8,128)(2,1)} %constant.26.clone) | copy-start | bytes 73732
  0.0 3.7 %copy-start.2 = (bf16[128,96]{1,0:T(8,128)(2,1)S(1)}, bf16[128,96]{1,0:T(8,128)(2,1)}, u32[]{:S(2)}) copy-start(bf16[128,96]{1,0:T(8,128)(2,1)} %constant.25.clone) | copy-start | bytes 73732

commit v3 on v2

--- a/solution.py
+++ b/solution.py
@@ -15,8 +15,9 @@
 NC = 4
 CY = 32 // NC
 CL = CY * 128
+EARLY = 3 * NC // 4
 KX = 16
-CLASSES = ((8, 12), (10, 12), (12, 12))
+CLASSES = ((6, 10), (8, 12), (9, 12), (12, 12))
 PITCH = 72
 MESH = pl.DeviceIdType.MESH
 F32 = jnp.float32
@@ -100,41 +101,52 @@
     n0 = to_lanes(r0, gb)
     n0_next = to_lanes(r0, prv)
     n1 = to_lanes(r1, gb)
-    load = to_lanes(r2, nxt) + n1 + n0
+    n2_prev = to_lanes(r2, nxt)
+    load = n2_prev + n1 + n0
     sub = lax.broadcasted_iota(jnp.int32, (128, 128), 0)
     lan = lax.broadcasted_iota(jnp.int32, (128, 128), 1)
+    sub1 = lax.broadcasted_iota(jnp.int32, (128, 1), 0)
+    lan1 = lax.broadcasted_iota(jnp.int32, (1, 128), 1)
     eye = sub == lan
 
     def to_rows(values):
         return jnp.sum(jnp.where(eye, values, 0.0), axis=1, keepdims=True)
 
-    low = -jnp.floor(n0_next * 0.5)
-    high = to_rows(n1 + jnp.floor((n0 + 1.0) * 0.5))
-    load_rows = to_rows(load)
-    is_edge = lax.rem((sub + 1) // 2, 2) == 0
+    low = -n0_next
+    high = to_rows(n1 + n0)
+    prev_rows = to_rows(n2_prev)
+    load_rows = jnp.where(sub < groups, to_rows(load), 0.0)
+    prefix = jnp.sum(jnp.where(sub <= lan, load_rows, 0.0), axis=0, keepdims=True)
+    total = jnp.sum(load_rows, axis=0, keepdims=True)
+    path = to_rows(prefix) - prefix + jnp.where(sub < lan, total, 0.0) + low
+    path = jnp.where(lan < groups, path, -1e9)
+
+    def edges_to(m):
+        return 2 * (m // 4) + 1 + lax.rem(m, 4) // 3
+
+    def held_to(m, edge, inner):
+        return (inner * (m + 1) + (edge - inner) * edges_to(m)).astype(F32)
+
+    is_edge = lax.rem((lax.rem(sub1, 4) + 1) // 2, 2) == 0
     choice, flow = None, None
     for index in reversed(range(len(classes))):
         edge, inner = classes[index]
-        excess = load_rows - jnp.where(is_edge, float(edge), float(inner))
-        excess = jnp.where(sub < groups, excess, 0.0)
-        prefix = jnp.sum(jnp.where(sub <= lan, excess, 0.0), axis=0, keepdims=True)
-        total = jnp.sum(excess, axis=0, keepdims=True)
-        path = to_rows(prefix) - prefix + jnp.where(sub < lan, total, 0.0) + low
-        need = jnp.max(jnp.where(lan < groups, path, -1e9), axis=1, keepdims=True)
+        held = float((edge + inner) * (groups // 2))
+        need = path - held_to(sub1, edge, inner) + held_to(lan1, edge, inner)
+        need = jnp.max(jnp.where(sub < lan, need - held, need), axis=1, keepdims=True)
         if choice is None:
             choice, flow = jnp.full((1, 1), float(index), F32), need
         else:
-            over = jnp.where(sub[:, :1] < groups, need - high, -1e9)
-            worst = jnp.maximum(jnp.max(over, axis=0, keepdims=True), total[:, :1])
+            over = jnp.maximum(need - high, prev_rows - jnp.where(is_edge, float(edge), float(inner)))
+            over = jnp.where(sub1 < groups, over, -1e9)
+            worst = jnp.maximum(jnp.max(over, axis=0, keepdims=True), total[:, :1] - held)
             fits = worst < 0.5
             choice = jnp.where(fits, float(index), choice)
             flow = jnp.where(fits, need, flow)
-    class_ref[...] = jnp.broadcast_to(choice, (8, 128)).astype(jnp.int32)
+    class_ref[0] = jnp.max(choice).astype(jnp.int32)
 
     left = jnp.where(group == 0, groups - 1, group - 1)
     right = jnp.where(group == groups - 1, 0, group + 1)
-    sub1 = lax.broadcasted_iota(jnp.int32, (128, 1), 0)
-    lan1 = lax.broadcasted_iota(jnp.int32, (1, 128), 1)
 
     def at_row(values, index):
         return jnp.sum(jnp.where(sub1 == index, values, 0.0), axis=0, keepdims=True)
@@ -209,10 +221,10 @@
         out_shape=(
             jax.ShapeDtypeStruct((slots, 128), jnp.int32),
             jax.ShapeDtypeStruct((2, 3 * ORB, slots, 128), F32),
-            jax.ShapeDtypeStruct((8, 128), jnp.int32),
+            jax.ShapeDtypeStruct((1,), jnp.int32),
         ),
         in_specs=[vmem] * 4,
-        out_specs=(vmem, vmem, vmem),
+        out_specs=(vmem, vmem, pl.BlockSpec(memory_space=pltpu.SMEM)),
         name="plan",
     )(pair_mask, jnp.asarray(table), jnp.asarray(same_kind), jnp.asarray(before))
 
@@ -241,11 +253,21 @@
     groups = lax.axis_size("band")
     band = lax.axis_index("band")
     me = lax.axis_index("grid")
-    on_edge = 1 - lax.rem((lax.rem(band, 4) + 1) // 2, 2)
-    halves = inner_slots // 2 + on_edge * (edge_slots // 2 - inner_slots // 2)
+    z = lax.rem(band, 4)
+    on_edge = 1 - lax.rem((z + 1) // 2, 2)
+    held = inner_slots + on_edge * (edge_slots - inner_slots)
     chip, core = me // 2, lax.rem(me, 2)
-    mine = (halves - core + 1) // 2
-    others = (halves + core) // 2
+
+    def slot_of(k, r):
+        return (
+            4 * r
+            + 2 * (core if k in (0, 2) else 1 - core)
+            + (chip if k in (0, 1) else 1 - chip)
+        )
+
+    def rounds_of(k):
+        return (held + 3 - slot_of(k, 0)) // 4
+
     left = lax.rem(band + groups - 1, groups)
     right = lax.rem(band + 1, groups)
     peers = {
@@ -340,31 +362,28 @@
     def lanes(y):
         return pl.ds(pl.multiple_of(y * 128, 128), 128)
 
-    def slot_of(k, r):
-        half = 2 * r + (core if k in (0, 2) else 1 - core)
-        return 2 * half + (chip if k in (0, 1) else 1 - chip)
-
-    def densities(c, r, targets):
-        ids = []
-        for k in targets:
-            slot = slot_of(k, r)
-            ids.append((k, tab[slot, 0], tab[slot, 1]))
+    def densities(c, r, k):
+        slot = slot_of(k, r)
+        i, j = tab[slot, 0], tab[slot, 1]
 
         def one_tile(y, carry):
-            for k, i, j in ids:
-                value = orbs[c][i, :, lanes(y)] * orbs[c][j, :, lanes(y)]
-                if k == 0:
-                    cube[r, c * CY + y, me] = value
-                else:
-                    rho[k - 1, r, c * CY + y] = value
+            value = orbs[c][i, :, lanes(y)] * orbs[c][j, :, lanes(y)]
+            if k == 0:
+                cube[r, c * CY + y, me] = value
+            else:
+                rho[k - 1, r, c * CY + y] = value
             return carry
 
-        lax.fori_loop(0, CY, one_tile, 0)
-        for k in targets:
-            if k:
-                x1(k, r, c).start()
-
-    order = [(0, 0), (0, 1), (1, 0), (2, 0), (1, 1), (3, 0), (2, 1), (3, 1)]
+        lax.fori_loop(0, CY, one_tile, 0, unroll=4)
+        if k:
+            x1(k, r, c).start()
+
+    order = []
+    for c in range(NC):
+        order.append((c, 0))
+        if c % 2 == 0:
+            order.append((c // 2, 1))
+    order += [(c, 1) for c in range((NC + 1) // 2, NC)]
     order += [(c, r) for r in range(2, rounds) for c in range(NC)]
     seen = set()
     for c, r in order:
@@ -375,13 +394,11 @@
             z1(0, c).wait_recv()
             z1(1, c).wait_recv()
 
-        @pl.when(r < mine)
-        def _():
-            densities(c, r, (2, 0))
-
-        @pl.when(r < others)
-        def _():
-            densities(c, r, (3, 1))
+        for k in (2, 3, 1, 0):
+
+            @pl.when(slot_of(k, r) < held)
+            def _():
+                densities(c, r, k)
 
     ax = ax_ref[...]
     wz = wz_ref[...]
@@ -437,6 +454,8 @@
         tiles = along_x(along_z(tiles))
         for t in range(CY):
             vout[r, c * CY + t] = tiles[t].reshape(4, 16, 128)
+
+    def return_chunk(r, c):
         for k in (2, 3, 1):
             x2(k, r, c).start()
 
@@ -447,58 +466,62 @@
 
         lax.fori_loop(0, count, body, 0)
 
-    @functools.partial(looped, mine)
+    @functools.partial(looped, rounds_of(0))
     def _(r):
         looped(NC, functools.partial(forward, r))
         looped(NG // KX, functools.partial(middle, r))
-        looped(NC, functools.partial(inverse, r))
+
+        @functools.partial(looped, NC)
+        def _(c):
+            inverse(r, c)
+
+            @pl.when((c < EARLY) | (r == rounds_of(0) - 1))
+            def _():
+                return_chunk(r, c)
+
+            @pl.when((c >= EARLY) & (r == rounds_of(0) - 1))
+            def _():
+                looped(r, lambda before: return_chunk(before, c))
 
     for c in range(NC):
         sums[c][...] = jnp.zeros_like(sums[c])
 
-    def accumulate(c, r, sources):
-        ids = []
-        for k in sources:
-            slot = slot_of(k, r)
-            ids.append((k, slot, tab[slot, 0], tab[slot, 1]))
-            if k:
-                x2(k, r, c).wait_recv()
+    def accumulate(c, r, k):
+        slot = slot_of(k, r)
+        i, j = tab[slot, 0], tab[slot, 1]
+        if k:
+            x2(k, r, c).wait_recv()
 
         @functools.partial(looped, CY)
         def _(y):
-            totals = [sums[c][q, :, lanes(y)] for q in range(3 * ORB)]
-            for k, slot, i, j in ids:
-                if k == 0:
-                    v = vout[r, c * CY + y, me]
-                else:
-                    v = vrecv[k - 1, r, c * CY + y]
-                on_i = v * orbs[c][j, :, lanes(y)]
-                on_j = v * orbs[c][i, :, lanes(y)]
-                for q in range(3 * ORB):
-                    totals[q] = totals[q] + (
-                        coef[0, q, pl.ds(slot, 1), :] * on_i
-                        + coef[1, q, pl.ds(slot, 1), :] * on_j
-                    )
+            if k == 0:
+                v = vout[r, c * CY + y, me]
+            else:
+                v = vrecv[k - 1, r, c * CY + y]
+            on_i = v * orbs[c][j, :, lanes(y)]
+            on_j = v * orbs[c][i, :, lanes(y)]
             for q in range(3 * ORB):
-                sums[c][q, :, lanes(y)] = totals[q]
+                sums[c][q, :, lanes(y)] += (
+                    coef[0, q, pl.ds(slot, 1), :] * on_i + coef[1, q, pl.ds(slot, 1), :] * on_j
+                )
 
     def both(c, r):
-        @pl.when(r < mine)
-        def _():
-            accumulate(c, r, (0, 2))
-
-        @pl.when(r < others)
-        def _():
-            accumulate(c, r, (1, 3))
-
-    last = (halves + 1) // 2 - 1
+        for k in (0, 1, 2, 3):
+
+            @pl.when(slot_of(k, r) < held)
+            def _():
+                accumulate(c, r, k)
+
+    last = (held + 3) // 4 - 1
 
     @functools.partial(looped, last)
     def _(r):
-        for c in range(NC):
+        for c in range(EARLY):
             both(c, r)
 
     for c in range(NC):
+        if c >= EARLY:
+            looped(last, functools.partial(both, c))
         both(c, last)
         z2(0, c).start()
         z2(1, c).start()
@@ -516,18 +539,18 @@
             z1(side, c).wait_send()
             z2(side, c).wait_send()
 
-    @functools.partial(looped, mine)
+    for k in (1, 2, 3):
+
+        @functools.partial(looped, rounds_of(k))
+        def _(r):
+            for c in range(NC):
+                x1(k, r, c).wait_send()
+
+    @functools.partial(looped, rounds_of(0))
     def _(r):
         for c in range(NC):
-            x1(2, r, c).wait_send()
             for k in (1, 2, 3):
                 x2(k, r, c).wait_send()
-
-    @functools.partial(looped, others)
-    def _(r):
-        for c in range(NC):
-            for k in (1, 3):
-                x1(k, r, c).wait_send()
 
 
 def mega(slots, collective_id, tab, coef, orbitals):
@@ -582,7 +605,7 @@
     branches = [functools.partial(mega, slots, 3 + n) for n, slots in enumerate(CLASSES)]
     if len(branches) == 1:
         return branches[0](tab, coef, orbitals)
-    return lax.switch(index[0, 0], branches, tab, coef, orbitals)
+    return lax.switch(index[0], branches, tab, coef, orbitals)
 
 
 def solution(mesh):

time: 106 us -> 97.4 us (0.919); the launches traced: 107 us -> 97.2 us
  Pallas kernels: 105 us -> 95.4 us
  local copies, waits for them, and re-layouts: 2.08 us -> 0.89 us
    pallas_call x1, Pallas kernels: 103 us -> 93.5 us  [mega(): pl.pallas_call(functools.partial(mega_kernel, *slots), out_shape=jax.Shap...]
    slice x1 -> x0, local copies, waits for them, and re-layouts: 1.19 us -> none  [local(): return lax.switch(index[0, 0], branches, tab, coef, orbitals)]
where the time goes in v3:
time: 97.4 us; the launch traced here: 97.2 us
  Pallas kernels  95.4 us (98%)
    pallas_call x1, Pallas kernels, mega(): pl.pallas_call(functools.partial(mega_kernel, *slots), out_shape=jax.Shap...  93.5 us

profile of v3, /device:TPU:1, one launch (start us, length us, event | category | flops | bytes accessed | tf_op | source)
XLA Modules:
  0.0 97.2 jit_solution(11615823786428179063)
XLA Ops:
  0.0 0.0 copy-start.2
  0.0 0.0 copy-start
  0.0 0.0 copy-start.1
  0.0 1.9 %plan.1 = (s32[16,128]{1,0:T(8,128)S(1)}, f32[2,9,16,128]{3,2,1,0:T(8,128)S(1)}, s32[1]{0:T(128)}) custom-call(s32[96,96]{1,0:T(8,128)} %mask_ref.1, s32[8,128]{1,0:T(8,128)} %constant.20.clone.cand_ref, f32[128,128]{1,0:T(8,128)} %constant.21.clone.same_ref, f32[128,128]{1,0:T(8,128)} %constant.22.clone.before_ref), custom_call_target="tpu_custom_call" | custom-call | tf_op jit(solution)/shard_map/plan/pallas_call | solution.py:219
  2.6 0.0 copy-done.2
  2.6 0.0 copy-done
  2.6 0.0 copy-done.1
  2.6 93.7 %conditional.1 = (f32[3,16,4096]{2,1,0:T(8,128)S(1)}) conditional(s32[]{:T(128)} %bitcast, (s32[16,128]{1,0:T(8,128)S(1)}, f32[2,9,16,128]{3,2,1,0:T(8,128)S(1)}, bf16[64,192]{1,0:T(8,128)(2,1)}, bf16[256,256]{1,0:T(8,128)(2,1)S(1)}, bf16[128,96]{1,0:T(8,128)(2,1)S(1)}, /*index=5*/bf16[128,96]{1,0:T(8,128)(2,1)S(1)}, ...), branch_computations={%region_0.0_spmd, %region_1.0_spmd, %region_2.0_spmd, %region_3.0_... | conditional | bytes 8 | solution.py:608
  2.6 93.5 %mega8_12.1 = f32[3,16,4096]{2,1,0:T(8,128)S(1)} custom-call(s32[16,128]{1,0:T(8,128)S(1)} %get-tuple-element.73.refs_0_, f32[2,9,16,128]{3,2,1,0:T(8,128)S(1)} %get-tuple-element.74.refs_1_, bf16[64,192]{1,0:T(8,128)(2,1)} %get-tuple-element.75.refs_2_, bf16[256,256]{1,0:T(8,128)(2,1)S(1)} %get-tuple-element.76.refs_3_, ...), custom_call_target="tpu_custom_call" | custom-call | tf_op jit(solution)/shard_map/cond/branch_1_fun/mega8_12/pallas_call | solution.py:562
  96.4 0.9 copy.31
Async XLA Ops:
  0.0 2.6 %copy-start.2 = (bf16[128,96]{1,0:T(8,128)(2,1)S(1)}, bf16[128,96]{1,0:T(8,128)(2,1)}, u32[]{:S(2)}) copy-start(bf16[128,96]{1,0:T(8,128)(2,1)} %constant.25.clone) | copy-start | bytes 73732
  0.0 2.6 %copy-start = (bf16[256,256]{1,0:T(8,128)(2,1)S(1)}, bf16[256,256]{1,0:T(8,128)(2,1)}, u32[]{:S(2)}) copy-start(bf16[256,256]{1,0:T(8,128)(2,1)} %constant.24.clone) | copy-start | bytes 393220
  0.0 2.6 %copy-start.1 = (bf16[128,96]{1,0:T(8,128)(2,1)S(1)}, bf16[128,96]{1,0:T(8,128)(2,1)}, u32[]{:S(2)}) copy-start(bf16[128,96]{1,0:T(8,128)(2,1)} %constant.26.clone) | copy-start | bytes 73732

commit v4 on v3

--- a/solution.py
+++ b/solution.py
@@ -15,9 +15,9 @@
 NC = 4
 CY = 32 // NC
 CL = CY * 128
-EARLY = 3 * NC // 4
+EARLY = NC // 2
 KX = 16
-CLASSES = ((6, 10), (8, 12), (9, 12), (12, 12))
+CLASSES = ((6, 10), (6, 11), (8, 12), (9, 12), (12, 12))
 PITCH = 72
 MESH = pl.DeviceIdType.MESH
 F32 = jnp.float32

time: 97.4 us -> 97.7 us (level)
  no operation moved by 1% of the time
where the time goes in v4:
time: 97.7 us; the launch traced here: 97.5 us
  Pallas kernels  95.5 us (98%)
    pallas_call x1, Pallas kernels, mega(): pl.pallas_call(functools.partial(mega_kernel, *slots), out_shape=jax.Shap...  93.6 us

profile of v4, /device:TPU:1, one launch (start us, length us, event | category | flops | bytes accessed | tf_op | source)
XLA Modules:
  0.0 97.5 jit_solution(16350300463425159744)
XLA Ops:
  0.0 0.0 copy-start.2
  0.0 0.0 copy-start
  0.0 0.0 copy-start.1
  0.0 1.9 %plan.1 = (s32[16,128]{1,0:T(8,128)S(1)}, f32[2,9,16,128]{3,2,1,0:T(8,128)S(1)}, s32[1]{0:T(128)}) custom-call(s32[96,96]{1,0:T(8,128)} %mask_ref.1, s32[8,128]{1,0:T(8,128)} %constant.20.clone.cand_ref, f32[128,128]{1,0:T(8,128)} %constant.21.clone.same_ref, f32[128,128]{1,0:T(8,128)} %constant.22.clone.before_ref), custom_call_target="tpu_custom_call" | custom-call | tf_op jit(solution)/shard_map/plan/pallas_call | solution.py:219
  2.6 0.0 copy-done.2
  2.6 0.0 copy-done
  2.6 0.0 copy-done.1
  2.6 94.0 %conditional.1 = (f32[3,16,4096]{2,1,0:T(8,128)S(1)}) conditional(s32[]{:T(128)} %bitcast, (s32[16,128]{1,0:T(8,128)S(1)}, f32[2,9,16,128]{3,2,1,0:T(8,128)S(1)}, bf16[64,192]{1,0:T(8,128)(2,1)}, bf16[256,256]{1,0:T(8,128)(2,1)S(1)}, bf16[128,96]{1,0:T(8,128)(2,1)S(1)}, /*index=5*/bf16[128,96]{1,0:T(8,128)(2,1)S(1)}, ...), branch_computations={%region_0.0_spmd, %region_1.0_spmd, %region_2.0_spmd, %region_3.0_... | conditional | bytes 8 | solution.py:608
  2.6 93.6 %mega8_12.1 = f32[3,16,4096]{2,1,0:T(8,128)S(1)} custom-call(s32[16,128]{1,0:T(8,128)S(1)} %get-tuple-element.95.refs_0_, f32[2,9,16,128]{3,2,1,0:T(8,128)S(1)} %get-tuple-element.96.refs_1_, bf16[64,192]{1,0:T(8,128)(2,1)} %get-tuple-element.97.refs_2_, bf16[256,256]{1,0:T(8,128)(2,1)S(1)} %get-tuple-element.98.refs_3_, ...), custom_call_target="tpu_custom_call" | custom-call | tf_op jit(solution)/shard_map/cond/branch_2_fun/mega8_12/pallas_call | solution.py:562
  96.6 0.9 copy.37
Async XLA Ops:
  0.0 2.6 %copy-start.2 = (bf16[128,96]{1,0:T(8,128)(2,1)S(1)}, bf16[128,96]{1,0:T(8,128)(2,1)}, u32[]{:S(2)}) copy-start(bf16[128,96]{1,0:T(8,128)(2,1)} %constant.25.clone) | copy-start | bytes 73732
  0.0 2.6 %copy-start = (bf16[256,256]{1,0:T(8,128)(2,1)S(1)}, bf16[256,256]{1,0:T(8,128)(2,1)}, u32[]{:S(2)}) copy-start(bf16[256,256]{1,0:T(8,128)(2,1)} %constant.24.clone) | copy-start | bytes 393220
  0.0 2.6 %copy-start.1 = (bf16[128,96]{1,0:T(8,128)(2,1)S(1)}, bf16[128,96]{1,0:T(8,128)(2,1)}, u32[]{:S(2)}) copy-start(bf16[128,96]{1,0:T(8,128)(2,1)} %constant.26.clone) | copy-start | bytes 73732

commit v5 on v4

--- a/solution.py
+++ b/solution.py
@@ -17,7 +17,7 @@
 CL = CY * 128
 EARLY = NC // 2
 KX = 16
-CLASSES = ((6, 10), (6, 11), (8, 12), (9, 12), (12, 12))
+CLASSES = ((6, 10), (7, 11), (8, 12), (9, 12), (12, 12))
 PITCH = 72
 MESH = pl.DeviceIdType.MESH
 F32 = jnp.float32
@@ -380,23 +380,25 @@
 
     order = []
     for c in range(NC):
-        order.append((c, 0))
+        order.append((c, 0, True, True))
         if c % 2 == 0:
-            order.append((c // 2, 1))
-    order += [(c, 1) for c in range((NC + 1) // 2, NC)]
-    order += [(c, r) for r in range(2, rounds) for c in range(NC)]
+            order.append((c // 2, 1, False, True))
+    order += [(c, 1, True, c >= (NC + 1) // 2) for c in range(NC)]
+    order += [(c, r, True, True) for r in range(2, rounds) for c in range(NC)]
     seen = set()
-    for c, r in order:
+    for c, r, at_edge, at_inner in order:
         if r >= rounds:
             continue
         if c not in seen:
             seen.add(c)
             z1(0, c).wait_recv()
             z1(1, c).wait_recv()
-
         for k in (2, 3, 1, 0):
-
-            @pl.when(slot_of(k, r) < held)
+            here = slot_of(k, r) < held
+            if not (at_edge and at_inner):
+                here &= on_edge == (1 if at_edge else 0)
+
+            @pl.when(here)
             def _():
                 densities(c, r, k)
 
@@ -475,13 +477,13 @@
         def _(c):
             inverse(r, c)
 
-            @pl.when((c < EARLY) | (r == rounds_of(0) - 1))
+            @pl.when((r < on_edge) | (c < EARLY) | (r == rounds_of(0) - 1))
             def _():
                 return_chunk(r, c)
 
             @pl.when((c >= EARLY) & (r == rounds_of(0) - 1))
             def _():
-                looped(r, lambda before: return_chunk(before, c))
+                looped(r - on_edge, lambda n: return_chunk(n + on_edge, c))
 
     for c in range(NC):
         sums[c][...] = jnp.zeros_like(sums[c])

time: 97.7 us -> 85.6 us (0.88)
  Pallas kernels: 95.5 us -> 83.6 us
    pallas_call x1, Pallas kernels: 93.6 us -> 81.6 us  [mega(): pl.pallas_call(functools.partial(mega_kernel, *slots), out_shape=jax.Shap...]
where the time goes in v5:
time: 85.6 us; the launch traced here: 85.4 us
  Pallas kernels  83.6 us (98%)
  local copies, waits for them, and re-layouts  0.89 us (1%)
    pallas_call x1, Pallas kernels, mega(): pl.pallas_call(functools.partial(mega_kernel, *slots), out_shape=jax.Shap...  81.6 us
    pallas_call x1, Pallas kernels, plan(): pl.pallas_call(functools.partial(plan_kernel, slots, classes), out_shape=...  1.92 us

profile of v5, /device:TPU:1, one launch (start us, length us, event | category | flops | bytes accessed | tf_op | source)
XLA Modules:
  0.0 85.4 jit_solution(97343881485013598)
XLA Ops:
  0.0 0.0 copy-start.2
  0.0 0.0 copy-start
  0.0 0.0 copy-start.1
  0.0 1.9 %plan.1 = (s32[16,128]{1,0:T(8,128)S(1)}, f32[2,9,16,128]{3,2,1,0:T(8,128)S(1)}, s32[1]{0:T(128)}) custom-call(s32[96,96]{1,0:T(8,128)} %mask_ref.1, s32[8,128]{1,0:T(8,128)} %constant.20.clone.cand_ref, f32[128,128]{1,0:T(8,128)} %constant.21.clone.same_ref, f32[128,128]{1,0:T(8,128)} %constant.22.clone.before_ref), custom_call_target="tpu_custom_call" | custom-call | tf_op jit(solution)/shard_map/plan/pallas_call | solution.py:219
  2.6 0.0 copy-done.2
  2.6 0.0 copy-done
  2.6 0.0 copy-done.1
  2.6 81.9 %conditional.1 = (f32[3,16,4096]{2,1,0:T(8,128)S(1)}) conditional(s32[]{:T(128)} %bitcast, (s32[16,128]{1,0:T(8,128)S(1)}, f32[2,9,16,128]{3,2,1,0:T(8,128)S(1)}, bf16[64,192]{1,0:T(8,128)(2,1)}, bf16[256,256]{1,0:T(8,128)(2,1)S(1)}, bf16[128,96]{1,0:T(8,128)(2,1)S(1)}, /*index=5*/bf16[128,96]{1,0:T(8,128)(2,1)S(1)}, ...), branch_computations={%region_0.0_spmd, %region_1.0_spmd, %region_2.0_spmd, %region_3.0_... | conditional | bytes 8 | solution.py:610
  2.6 81.6 %mega6_10.1 = f32[3,16,4096]{2,1,0:T(8,128)S(1)} custom-call(s32[16,128]{1,0:T(8,128)S(1)} %get-tuple-element.70.refs_0_, f32[2,9,16,128]{3,2,1,0:T(8,128)S(1)} %get-tuple-element.80.refs_1_, bf16[64,192]{1,0:T(8,128)(2,1)} %get-tuple-element.82.refs_2_, bf16[256,256]{1,0:T(8,128)(2,1)S(1)} %get-tuple-element.84.refs_3_, ...), custom_call_target="tpu_custom_call" | custom-call | tf_op jit(solution)/shard_map/cond/branch_0_fun/mega6_10/pallas_call | solution.py:564
  84.5 0.9 %copy.37 = f32[3,16,4096]{2,1,0:T(8,128)} copy(f32[3,16,4096]{2,1,0:T(8,128)S(1)} %get-tuple-element.122) | data formatting | bytes 1572864
Async XLA Ops:
  0.0 2.6 %copy-start.2 = (bf16[128,96]{1,0:T(8,128)(2,1)S(1)}, bf16[128,96]{1,0:T(8,128)(2,1)}, u32[]{:S(2)}) copy-start(bf16[128,96]{1,0:T(8,128)(2,1)} %constant.25.clone) | copy-start | bytes 73732
  0.0 2.6 %copy-start = (bf16[256,256]{1,0:T(8,128)(2,1)S(1)}, bf16[256,256]{1,0:T(8,128)(2,1)}, u32[]{:S(2)}) copy-start(bf16[256,256]{1,0:T(8,128)(2,1)} %constant.24.clone) | copy-start | bytes 393220
  0.0 2.6 %copy-start.1 = (bf16[128,96]{1,0:T(8,128)(2,1)S(1)}, bf16[128,96]{1,0:T(8,128)(2,1)}, u32[]{:S(2)}) copy-start(bf16[128,96]{1,0:T(8,128)(2,1)} %constant.26.clone) | copy-start | bytes 73732
